TPU v7x, 512 devices: a whole 4x8x8 slice. The times are simulated.
512 devices in a mesh: grp: 16 (over z, core), shard: 32 (over x, y).
Axes of the slice: x: 4, y: 8, z: 8, core: 2. Of those that a mesh axis runs over, the one named last changes fastest.
Arguments:
- partial_grads: bfloat16 [16, 4096, 6144], P('grp', 'shard')
- joined_block: int32 [48], replicated, may hold values from 0 to 47, each once
- head_slot: int32 [48], replicated, may hold values from 0 to 63, as said below
Outputs:
- head_grads: float32 [64, 32, 128, 128], P('shard', None, 'grp')
- head_rms: float32 [64], P('shard')
- type_rms: float32 [3], replicated
Inputs may be any that keep to these rules, and one draw needn't show every extreme that they name: `joined_block`: a permutation: each block number appears once. `head_slot`: distinct slots; every owner along shard holds 2 or 1 head blocks, and some owner holds 2.
All inputs are finite; a program needn't handle non-finite values.
Results may differ from a plain program's by a relative error of at most 0.0003.
Values may be sent and summed in bfloat16 or wider, within the bound.
No kernel may reach another device: no remote copies, remote signals or barrier semaphores. Data moves between devices by JAX's collectives and lax.ppermute only.
A program may use at most 64 MiB of HBM per device.

v0:
```python
import jax
import jax.numpy as jnp
from jax import lax
from jax.sharding import Mesh
from jax.sharding import PartitionSpec as P

D = 4096
QH = 32
KVH = 8
HS = 128
SHARD = ("shard_0", "shard_1")
GRP = ("grp_0", "grp_1")


def in_blocks(shard, dim, size):
    before, after = (shard.shape[:dim], shard.shape[dim + 1 :])
    return jnp.moveaxis(shard.reshape(*before, size, -1, *after), dim, 0)


def sent_and_summed(shard, axis, dim):
    size = lax.axis_size(axis)
    parts = lax.all_to_all(in_blocks(shard, dim, size), axis, 0, 0, tiled=True)
    return jnp.sum(parts, axis=0)


def summed_rows(shard, axes, dim):
    far, near = axes
    parts = in_blocks(shard, dim, lax.axis_size(far))
    nearer = sent_and_summed(parts, near, dim + 1)
    arrived = lax.all_to_all(nearer, far, split_axis=0, concat_axis=0, tiled=True)
    return arrived.sum(axis=0)


def sent_to_all(shard, axis):
    copies = jnp.broadcast_to(shard, (lax.axis_size(axis), *shard.shape))
    return lax.all_to_all(copies, axis, split_axis=0, concat_axis=0, tiled=True)


def over_copies(shard, axis):
    return sent_to_all(shard, axis).sum(axis=0)


def by_axis(shard, axes):
    far, near = axes
    return over_copies(over_copies(shard, near), far)


def per_device(partial_grads, joined_block, head_slot):
    own_rows = partial_grads[0]
    blocks = joined_block.shape[0]
    head_width = own_rows.shape[1] // blocks
    shard_count = lax.axis_size(SHARD)
    slots_dev = (blocks + shard_count - 1) // shard_count
    slot_total = slots_dev * shard_count
    first_slot = lax.axis_index(SHARD) * slots_dev
    block_ids = jnp.arange(blocks, dtype=jnp.int32)
    block_kind = (block_ids >= QH).astype(jnp.int32) + (block_ids >= QH + KVH).astype(jnp.int32)
    matches = (head_slot[None, :] == jnp.arange(slot_total, dtype=jnp.int32)[:, None]).astype(
        jnp.int32
    )
    occupied = jnp.sum(matches, axis=1)
    source = jnp.sum(matches * joined_block[None, :], axis=1)
    slot_kind = jnp.sum(matches * block_kind[None, :], axis=1) + (1 - occupied) * 3
    kind_ids = jnp.arange(3, dtype=jnp.int32)
    summed = summed_rows(own_rows.astype(jnp.float32), ("grp_0", "grp_1"), 0)
    picked = jnp.take(summed.reshape(summed.shape[0], blocks, head_width), source, axis=1)
    picked = jnp.where(occupied[None, :, None] > 0, picked, jnp.zeros_like(picked))
    owned_block = lax.all_to_all(
        jnp.transpose(picked, (1, 0, 2))[:, None], SHARD, split_axis=0, concat_axis=1, tiled=True
    )
    joined_squares = jnp.sum(
        (summed * summed).reshape(summed.shape[0], blocks, head_width), axis=(0, 2)
    )
    local_squares = joined_squares[source] * occupied.astype(jnp.float32)
    every_square = by_axis(local_squares, (("grp_0", "grp_1"), ("shard_0", "shard_1")))
    head_squares = lax.dynamic_slice(every_square, (first_slot,), (slots_dev,))
    selector = (slot_kind[:, None] == kind_ids[None, :]).astype(jnp.float32)
    type_squares = jnp.sum(every_square[:, None] * selector, axis=0)
    head_rms = jnp.sqrt(head_squares / (D * HS))
    counts = jnp.array([QH, KVH, KVH], jnp.float32) * (D * HS)
    type_rms = jnp.sqrt(type_squares / counts)
    return (owned_block, head_rms, type_rms)


def solution(mesh):
    finer = Mesh(mesh.devices.reshape(8, 2, 4, 8), ("grp_0", "grp_1", "shard_0", "shard_1"))
    in_specs = (P(GRP, SHARD, None), P(), P())
    out_specs = (P(SHARD, None, GRP, None), P(SHARD), P())
    return jax.shard_map(
        per_device, mesh=finer, in_specs=in_specs, out_specs=out_specs, check_vma=False
    )
```

profile of v0, /device:TPU:8, one launch (start us, length us, event | category | flops | bytes accessed | tf_op | source)
XLA Modules:
  0.0 111.5 jit_solution(73931022079895481)
XLA Ops:
  0.6 1.7 %convert_bitcast_fusion = f32[2,8,8,6144]{3,2,0,1:T(8,128)S(1)} fusion(bf16[8,2,8,6144]{3,2,1,0:T(8,128)(2,1)} %bitcast.21), kind=kLoop, calls=%fused_computation.2 | loop fusion | flops 786432 | bytes 4718592 | tf_op jit(solution)/shard_map/transpose | solution.py:17
  2.3 0.3 copy.13
  2.6 6.3 %all_to_all.40 = f32[2,8,8,6144]{3,2,1,0:T(8,128)S(1)} all-to-all(f32[2,8,8,6144]{3,2,1,0:T(8,128)S(1)} %copy.13), channel_id=1, replica_groups=mesh['grp_0'=8,'grp_1'=2,'shard_0'=4,'shard_1'=8] {'grp_1'}, dimensions={0} | all-to-all | bytes 6291456 | tf_op jit(solution)/shard_map/all_to_all | solution.py:22
  8.9 0.0 copy-start
  8.9 0.0 copy-start.1
  8.9 1.5 %reduce_sum.92 = f32[8,8,6144]{2,1,0:T(8,128)} reduce(f32[2,8,8,6144]{3,2,1,0:T(8,128)S(1)} %all_to_all.40, f32[]{:T(128)} %constant.20.clone.1), dimensions={0}, to_apply=%region_2.0 | reduce | flops 393216 | bytes 4718596 | tf_op jit(solution)/shard_map/reduce_sum | solution.py:23
  10.4 0.0 copy-start.2
  10.4 10.4 %all-to-all-start.1 = ((f32[8,8,6144]{2,1,0:T(8,128)}), f32[8,8,6144]{2,1,0:T(8,128)S(1)}, u32[]{:S(2)}, u32[]{:S(2)}) async-start(f32[8,8,6144]{2,1,0:T(8,128)} %reduce_sum.92), calls=%async_computation.1 | async-start | bytes 3145728 | tf_op jit(solution)/shard_map/all_to_all | solution.py:30
  20.9 0.0 copy-done
  20.9 0.0 copy-done.1
  20.9 0.1 select_reduce_fusion
  21.0 40.1 %all-to-all-done.1 = f32[8,8,6144]{2,1,0:T(8,128)S(1)} async-done(((f32[8,8,6144]{2,1,0:T(8,128)}), f32[8,8,6144]{2,1,0:T(8,128)S(1)}, u32[]{:S(2)}, u32[]{:S(2)}) %all-to-all-start.1) | async-done | bytes 1572896 | tf_op jit(solution)/shard_map/all_to_all | solution.py:30
  61.1 0.1 reduce_sum.93
  61.2 0.1 multiply_reduce_fusion
  61.3 0.1 bitcast_reduce_fusion
  61.4 0.8 gather_fusion.1
  62.2 0.6 broadcast_in_dim.44
  62.8 10.2 %all-to-all-start.3 = ((f32[32,1,64]{2,1,0:T(1,128)}), f32[32,1,64]{2,1,0:T(1,128)S(1)}, u32[]{:S(2)}, u32[]{:S(2)}) async-start(f32[32,1,64]{2,1,0:T(1,128)} %broadcast_in_dim.44), calls=%async_computation.3 | async-start | bytes 32768 | tf_op jit(solution)/shard_map/all_to_all | solution.py:36
  73.0 0.6 gather_fusion
  73.6 7.9 %all-to-all-done.3 = f32[32,1,64]{2,1,0:T(1,128)S(1)} async-done(((f32[32,1,64]{2,1,0:T(1,128)}), f32[32,1,64]{2,1,0:T(1,128)S(1)}, u32[]{:S(2)}, u32[]{:S(2)}) %all-to-all-start.3) | async-done | bytes 8224 | tf_op jit(solution)/shard_map/all_to_all | solution.py:36
  81.6 0.6 broadcast_in_dim.45
  82.2 3.5 %all-to-all-start.4 = ((f32[16,1,64]{2,1,0:T(1,128)}), f32[16,1,64]{2,1,0:T(1,128)S(1)}, u32[]{:S(2)}, u32[]{:S(2)}) async-start(f32[16,1,64]{2,1,0:T(1,128)} %broadcast_in_dim.45), calls=%async_computation.4 | async-start | bytes 16384 | tf_op jit(solution)/shard_map/all_to_all | solution.py:36
  85.7 0.9 select_bitcast_fusion
  86.6 6.6 %all-to-all-done.4 = f32[16,1,64]{2,1,0:T(1,128)S(1)} async-done(((f32[16,1,64]{2,1,0:T(1,128)}), f32[16,1,64]{2,1,0:T(1,128)S(1)}, u32[]{:S(2)}, u32[]{:S(2)}) %all-to-all-start.4) | async-done | bytes 4128 | tf_op jit(solution)/shard_map/all_to_all | solution.py:36
  93.2 4.9 %all-to-all-start.2 = ((f32[64,1,8,128]{3,2,1,0:T(8,128)}), f32[64,1,8,128]{3,2,1,0:T(8,128)S(1)}, u32[]{:S(2)}, u32[]{:S(2)}) async-start(f32[64,1,8,128]{3,2,1,0:T(8,128)} %select_bitcast_fusion), calls=%async_computation.2 | async-start | bytes 524288 | tf_op jit(solution)/shard_map/all_to_all | solution.py:68
  98.2 0.6 multiply_sqrt_fusion.1
  98.8 0.1 select_reduce_fusion.2
  98.9 0.0 copy-done.2
  98.9 0.5 multiply_sqrt_fusion
  99.4 11.4 %all-to-all-done.2 = f32[64,1,8,128]{3,2,1,0:T(8,128)S(1)} async-done(((f32[64,1,8,128]{3,2,1,0:T(8,128)}), f32[64,1,8,128]{3,2,1,0:T(8,128)S(1)}, u32[]{:S(2)}, u32[]{:S(2)}) %all-to-all-start.2) | async-done | bytes 262176 | tf_op jit(solution)/shard_map/all_to_all | solution.py:68
  110.8 0.7 copy.16
  (8 shorter events, 0.1 us)
Async XLA Ops:
  8.9 12.0 %copy-start = (s32[48]{0:T(128)S(1)}, s32[48]{0:T(128)}, u32[]{:S(2)}) copy-start(s32[48]{0:T(128)} %param.6) | copy-start | bytes 580
  8.9 12.0 %copy-start.1 = (s32[48]{0:T(128)S(1)}, s32[48]{0:T(128)}, u32[]{:S(2)}) copy-start(s32[48]{0:T(128)} %param.5) | copy-start | bytes 580
  10.4 88.5 %copy-start.2 = (f32[3]{0:T(128)S(1)}, f32[3]{0:T(128)}, u32[]{:S(2)}) copy-start(f32[3]{0:T(128)} %constant.58) | copy-start | bytes 40
  10.4 50.7 %all-to-all-start.1 = ((f32[8,8,6144]{2,1,0:T(8,128)}), f32[8,8,6144]{2,1,0:T(8,128)S(1)}, u32[]{:S(2)}, u32[]{:S(2)}) async-start(f32[8,8,6144]{2,1,0:T(8,128)} %reduce_sum.92), calls=%async_computation.1 | async-start | bytes 3145728 | tf_op jit(solution)/shard_map/all_to_all | solution.py:30
  62.8 18.7 %all-to-all-start.3 = ((f32[32,1,64]{2,1,0:T(1,128)}), f32[32,1,64]{2,1,0:T(1,128)S(1)}, u32[]{:S(2)}, u32[]{:S(2)}) async-start(f32[32,1,64]{2,1,0:T(1,128)} %broadcast_in_dim.44), calls=%async_computation.3 | async-start | bytes 32768 | tf_op jit(solution)/shard_map/all_to_all | solution.py:36
  82.2 11.0 %all-to-all-start.4 = ((f32[16,1,64]{2,1,0:T(1,128)}), f32[16,1,64]{2,1,0:T(1,128)S(1)}, u32[]{:S(2)}, u32[]{:S(2)}) async-start(f32[16,1,64]{2,1,0:T(1,128)} %broadcast_in_dim.45), calls=%async_computation.4 | async-start | bytes 16384 | tf_op jit(solution)/shard_map/all_to_all | solution.py:36
  93.2 17.6 %all-to-all-start.2 = ((f32[64,1,8,128]{3,2,1,0:T(8,128)}), f32[64,1,8,128]{3,2,1,0:T(8,128)S(1)}, u32[]{:S(2)}, u32[]{:S(2)}) async-start(f32[64,1,8,128]{3,2,1,0:T(8,128)} %select_bitcast_fusion), calls=%async_computation.2 | async-start | bytes 524288 | tf_op jit(solution)/shard_map/all_to_all | solution.py:68
where the time goes:
time: 112 us
  waiting for transfers between devices  66 us (59%)
  starting transfers between devices  29 us (26%)
  blocking collectives  6.26 us (6%)
  other arithmetic  5.78 us (5%)
  local copies, waits for them, and re-layouts  3.65 us (3%)
    all_to_all x1, waiting for transfers between devices, summed_rows(): lax.all_to_all(nearer, far, split_axis=0, concat_axis=0, tiled=True)  40.1 us
    all_to_all x2, waiting for transfers between devices, sent_to_all(): return lax.all_to_all(copies, axis, split_axis=0, concat_axis=0, tiled=True)  14.5 us
    all_to_all x2, starting transfers between devices, sent_to_all(): return lax.all_to_all(copies, axis, split_axis=0, concat_axis=0, tiled=True)  13.7 us
    all_to_all x1, waiting for transfers between devices, per_device(): lax.all_to_all(jnp.transpose(picked, (1, 0, 2))[:, None], SHARD, split_ax...  11.4 us
    all_to_all x1, starting transfers between devices, summed_rows(): lax.all_to_all(nearer, far, split_axis=0, concat_axis=0, tiled=True)  10.4 us
    all_to_all x1, blocking collectives, sent_and_summed(): parts = lax.all_to_all(in_blocks(shard, dim, size), axis, 0, 0, tiled=True)  6.26 us
    all_to_all x1, starting transfers between devices, per_device(): lax.all_to_all(jnp.transpose(picked, (1, 0, 2))[:, None], SHARD, split_ax...  4.93 us
  transfers between devices with their start and end apart: 4, of which 4 were waited for; matrix products, arithmetic and copies ran while one was open for 3% of the time, Pallas kernels for 0%

commit v1 on v0

v1 whole, which is shorter than its diff:
```python
import jax
import jax.numpy as jnp
from jax import lax
from jax.sharding import Mesh
from jax.sharding import PartitionSpec as P

D = 4096
QH = 32
KVH = 8
HS = 128
SHARD = ("shard_0", "shard_1")
GRP = ("grp_0", "grp_1")


def over_copies(row, axes):
    copies = jnp.broadcast_to(row, (lax.axis_size(axes), *row.shape))
    return lax.all_to_all(copies, axes, split_axis=0, concat_axis=0, tiled=True).sum(axis=0)


def per_device(partial_grads, joined_block, head_slot):
    own_rows = partial_grads[0]
    blocks = joined_block.shape[0]
    groups = lax.axis_size(GRP)
    width = own_rows.shape[1]
    rows = own_rows.shape[0] // groups
    shard_count = lax.axis_size(SHARD)
    slots_dev = (blocks + shard_count - 1) // shard_count
    slot_total = slots_dev * shard_count
    first_slot = lax.axis_index(SHARD) * slots_dev

    parts = lax.all_to_all(own_rows.reshape(groups, rows, width), GRP, 0, 0, tiled=True)
    summed = jnp.sum(parts.astype(jnp.float32), axis=0)

    by_block = summed.reshape(rows, blocks, HS)
    squares = jnp.sum(by_block * by_block, axis=(0, 2))
    square_tile = jnp.pad(squares[None], ((0, rows - 1), (0, HS - blocks)))

    block_ids = jnp.arange(blocks, dtype=jnp.int32)
    slot_ids = jnp.arange(slot_total, dtype=jnp.int32)
    matches = (head_slot[None, :] == slot_ids[:, None]).astype(jnp.int32)
    occupied = jnp.sum(matches, axis=1)
    source = jnp.sum(matches * joined_block[None, :], axis=1)
    picked = jnp.take(by_block, source, axis=1)
    picked = jnp.where(occupied[None, :, None] > 0, picked, jnp.zeros_like(picked))
    tiles = jnp.transpose(picked, (1, 0, 2)).reshape(shard_count, slots_dev, rows, HS)
    riders = jnp.broadcast_to(square_tile, (shard_count, 1, rows, HS))
    arrived = lax.all_to_all(
        jnp.concatenate([tiles, riders], axis=1), SHARD, split_axis=0, concat_axis=0, tiled=True
    )
    owned_block = jnp.transpose(arrived[:, :slots_dev], (1, 0, 2, 3))
    shard_squares = arrived[:, slots_dev, :1].sum(axis=0)

    every_square = over_copies(shard_squares, GRP)[0, :blocks]
    kind = (block_ids >= QH).astype(jnp.int32) + (block_ids >= QH + KVH).astype(jnp.int32)
    own = head_slot[None, :] == first_slot + jnp.arange(slots_dev, dtype=jnp.int32)[:, None]
    alike = kind[None, :] == jnp.arange(3, dtype=jnp.int32)[:, None]
    wanted = jnp.concatenate([own, alike], axis=0)
    joined = joined_block[:, None] == block_ids[None, :]
    chosen = jnp.any(wanted[:, :, None] & joined[None], axis=1).astype(jnp.float32)
    sums = jnp.sum(chosen * every_square[None, :], axis=1)
    head_rms = jnp.sqrt(sums[:slots_dev] / (D * HS))
    counts = jnp.array([QH, KVH, KVH], jnp.float32) * (D * HS)
    type_rms = jnp.sqrt(sums[slots_dev:] / counts)
    return (owned_block, head_rms, type_rms)


def solution(mesh):
    finer = Mesh(mesh.devices.reshape(8, 2, 4, 8), ("grp_0", "grp_1", "shard_0", "shard_1"))
    in_specs = (P(GRP, SHARD, None), P(), P())
    out_specs = (P(SHARD, None, GRP, None), P(SHARD), P())
    return jax.shard_map(
        per_device, mesh=finer, in_specs=in_specs, out_specs=out_specs, check_vma=False
    )
```

time: 112 us -> 91.2 us (0.81)
  blocking collectives: 6.26 us -> 0 us
  waiting for transfers between devices: 66 us -> 60.2 us
  starting transfers between devices: 29 us -> 24.8 us
  other arithmetic: 5.78 us -> 3.06 us
  local copies, waits for them, and re-layouts: 3.65 us -> 2.01 us
    all_to_all x1 -> x0, blocking collectives: 6.26 us -> none  [sent_and_summed(): parts = lax.all_to_all(in_blocks(shard, dim, size), axis, 0, 0, tiled=True)]
    all_to_all x4 -> x3, waiting for transfers between devices: 66 us -> 60.2 us  [the longest x1 37.7 us: per_device(): lax.all_to_all(own_rows.reshape(groups, rows, width), GRP, 0, 0, tiled=True)]
    all_to_all x4 -> x3, starting transfers between devices: 29 us -> 24.8 us  [the longest x1 10.6 us: per_device(): lax.all_to_all(own_rows.reshape(groups, rows, width), GRP, 0, 0, tiled=True)]
    transpose x1 -> x0, other arithmetic: 1.71 us -> none  [in_blocks(): return jnp.moveaxis(shard.reshape(*before, size, -1, *after), dim, 0)]
    reduce_sum x8 -> x7, other arithmetic: 2.01 us -> 0.66 us  [the longest x1 0.22 us: per_device(): summed = jnp.sum(parts.astype(jnp.float32), axis=0)]
  transfers between devices with their start and end apart: 4 -> 3, of which waited for: 4 -> 3; matrix products, arithmetic and copies ran while one was open for 3% -> 1% of each run, Pallas kernels for 0% -> 0%
where the time goes in v1:
time: 91.2 us; the launch traced here: 90.9 us
  waiting for transfers between devices  60.2 us (66%)
  starting transfers between devices  24.8 us (27%)
  other arithmetic  3.06 us (3%)
  local copies, waits for them, and re-layouts  2.01 us (2%)
    all_to_all x1, waiting for transfers between devices, per_device(): lax.all_to_all(own_rows.reshape(groups, rows, width), GRP, 0, 0, tiled=True)  37.7 us
    all_to_all x1, waiting for transfers between devices, per_device(): lax.all_to_all(jnp.concatenate([tiles, riders], axis=1), SHARD, split_axi...  15.7 us
    all_to_all x1, starting transfers between devices, per_device(): lax.all_to_all(own_rows.reshape(groups, rows, width), GRP, 0, 0, tiled=True)  10.6 us
    all_to_all x1, starting transfers between devices, per_device(): lax.all_to_all(jnp.concatenate([tiles, riders], axis=1), SHARD, split_axi...  10.2 us
    all_to_all x1, waiting for transfers between devices, over_copies(): lax.all_to_all(copies, axes, split_axis=0, concat_axis=0, tiled=True)  6.84 us
    all_to_all x1, starting transfers between devices, over_copies(): lax.all_to_all(copies, axes, split_axis=0, concat_axis=0, tiled=True)  4.07 us
  transfers between devices with their start and end apart: 3, of which 3 were waited for; matrix products, arithmetic and copies ran while one was open for 1% of the time, Pallas kernels for 0%

profile of v1, /device:TPU:8, one launch (start us, length us, event | category | flops | bytes accessed | tf_op | source)
XLA Modules:
  0.0 90.9 jit_solution(12536516205557448117)
XLA Ops:
  0.6 0.0 copy-start
  0.6 0.0 copy-start.1
  0.7 10.6 %all-to-all-start = ((bf16[16,8,6144]{2,1,0:T(8,128)(2,1)}), bf16[16,8,6144]{2,1,0:T(8,128)(2,1)S(1)}, u32[]{:S(2)}, u32[]{:S(2)}) async-start(bf16[16,8,6144]{2,1,0:T(8,128)(2,1)} %bitcast.17), calls=%async_computation | async-start | bytes 3145728 | tf_op jit(solution)/shard_map/all_to_all | solution.py:31
  11.2 0.0 copy-done
  11.2 0.0 copy-done.1
  11.3 0.1 convert_reduce_fusion.1
  11.4 37.7 %all-to-all-done = bf16[16,8,6144]{2,1,0:T(8,128)(2,1)S(1)} async-done(((bf16[16,8,6144]{2,1,0:T(8,128)(2,1)}), bf16[16,8,6144]{2,1,0:T(8,128)(2,1)S(1)}, u32[]{:S(2)}, u32[]{:S(2)}) %all-to-all-start) | async-done | bytes 1572896 | tf_op jit(solution)/shard_map/all_to_all | solution.py:31
  49.1 0.2 convert_reduce_fusion
  49.3 0.1 multiply_reduce_fusion
  49.4 0.1 bitcast_reduce_fusion
  49.5 0.6 gather_fusion
  50.1 0.0 copy-start.2
  50.1 0.2 select_select_fusion
  50.4 0.8 pad_maximum_fusion
  51.1 10.2 %all-to-all-start.1 = ((f32[32,3,8,128]{3,2,1,0:T(8,128)}), f32[32,3,8,128]{3,2,1,0:T(8,128)S(1)}, u32[]{:S(2)}, u32[]{:S(2)}) async-start(f32[32,3,8,128]{3,2,1,0:T(8,128)} %pad_maximum_fusion), calls=%async_computation.1 | async-start | bytes 786432 | tf_op jit(solution)/shard_map/all_to_all | solution.py:47
  61.3 0.1 broadcast_compare_fusion
  61.4 0.1 iota_compare_fusion
  61.5 0.1 and_reduce_fusion
  61.6 15.7 %all-to-all-done.1 = f32[32,3,8,128]{3,2,1,0:T(8,128)S(1)} async-done(((f32[32,3,8,128]{3,2,1,0:T(8,128)}), f32[32,3,8,128]{3,2,1,0:T(8,128)S(1)}, u32[]{:S(2)}, u32[]{:S(2)}) %all-to-all-start.1) | async-done | bytes 393248 | tf_op jit(solution)/shard_map/all_to_all | solution.py:47
  77.3 0.6 broadcast_in_dim.48
  77.9 4.1 %all-to-all-start.2 = ((f32[16,1,128]{2,1,0:T(1,128)}), f32[16,1,128]{2,1,0:T(1,128)S(1)}, u32[]{:S(2)}, u32[]{:S(2)}) async-start(f32[16,1,128]{2,1,0:T(1,128)} %broadcast_in_dim.48), calls=%async_computation.2 | async-start | bytes 16384 | tf_op jit(solution)/shard_map/all_to_all | solution.py:17
  82.1 0.7 copy.10
  82.8 6.8 %all-to-all-done.2 = f32[16,1,128]{2,1,0:T(1,128)S(1)} async-done(((f32[16,1,128]{2,1,0:T(1,128)}), f32[16,1,128]{2,1,0:T(1,128)S(1)}, u32[]{:S(2)}, u32[]{:S(2)}) %all-to-all-start.2) | async-done | bytes 8224 | tf_op jit(solution)/shard_map/all_to_all | solution.py:17
  89.6 0.1 select_reduce_fusion.1
  89.8 0.5 multiply_sqrt_fusion.1
  90.3 0.0 copy-done.2
  90.3 0.6 multiply_sqrt_fusion
  (13 shorter events, 0.2 us)
Async XLA Ops:
  0.6 10.6 %copy-start = (s32[48]{0:T(128)S(1)}, s32[48]{0:T(128)}, u32[]{:S(2)}) copy-start(s32[48]{0:T(128)} %param.5) | copy-start | bytes 580
  0.6 10.6 %copy-start.1 = (s32[48]{0:T(128)S(1)}, s32[48]{0:T(128)}, u32[]{:S(2)}) copy-start(s32[48]{0:T(128)} %param.6) | copy-start | bytes 580
  0.7 48.4 %all-to-all-start = ((bf16[16,8,6144]{2,1,0:T(8,128)(2,1)}), bf16[16,8,6144]{2,1,0:T(8,128)(2,1)S(1)}, u32[]{:S(2)}, u32[]{:S(2)}) async-start(bf16[16,8,6144]{2,1,0:T(8,128)(2,1)} %bitcast.17), calls=%async_computation | async-start | bytes 3145728 | tf_op jit(solution)/shard_map/all_to_all | solution.py:31
  50.1 40.2 %copy-start.2 = (f32[3]{0:T(128)S(1)}, f32[3]{0:T(128)}, u32[]{:S(2)}) copy-start(f32[3]{0:T(128)} %constant.54) | copy-start | bytes 40
  51.1 26.2 %all-to-all-start.1 = ((f32[32,3,8,128]{3,2,1,0:T(8,128)}), f32[32,3,8,128]{3,2,1,0:T(8,128)S(1)}, u32[]{:S(2)}, u32[]{:S(2)}) async-start(f32[32,3,8,128]{3,2,1,0:T(8,128)} %pad_maximum_fusion), calls=%async_computation.1 | async-start | bytes 786432 | tf_op jit(solution)/shard_map/all_to_all | solution.py:47
  77.9 11.7 %all-to-all-start.2 = ((f32[16,1,128]{2,1,0:T(1,128)}), f32[16,1,128]{2,1,0:T(1,128)S(1)}, u32[]{:S(2)}, u32[]{:S(2)}) async-start(f32[16,1,128]{2,1,0:T(1,128)} %broadcast_in_dim.48), calls=%async_computation.2 | async-start | bytes 16384 | tf_op jit(solution)/shard_map/all_to_all | solution.py:17

commit v2 on v1

v2 whole, which is shorter than its diff:
```python
import functools

import jax
import jax.numpy as jnp
from jax import lax
from jax.experimental import pallas as pl
from jax.experimental.pallas import tpu as pltpu
from jax.sharding import Mesh
from jax.sharding import PartitionSpec as P

D = 4096
QH = 32
KVH = 8
HS = 128
SHARD = ("shard_0", "shard_1")
GRP = ("grp_0", "grp_1")
IN_VMEM = pl.BlockSpec(memory_space=pltpu.VMEM)
PARAMS = pltpu.CompilerParams(vmem_limit_bytes=4 * 2**20)
IN_SMEM = pl.BlockSpec(memory_space=pltpu.SMEM)


def outgoing_body(peers, per_peer, source_ref, occupied_ref, summed_ref, out_ref):
    rows = summed_ref.shape[0]
    stride = per_peer * rows + 1
    slot_rows = []
    for slot in range(peers * per_peer):
        first = pl.multiple_of(source_ref[slot] * HS, HS)
        tile = summed_ref[:, pl.ds(first, HS)]
        tile = jnp.where(occupied_ref[slot] > 0, tile, jnp.zeros_like(tile))
        peer, nth = divmod(slot, per_peer)
        out_ref[pl.ds(peer * stride + nth * rows, rows), :] = tile
        slot_rows.append(jnp.sum(tile * tile, axis=0, keepdims=True))
    squares = jnp.sum(jnp.concatenate(slot_rows, axis=0), axis=1, keepdims=True)
    shape = (peers * per_peer, HS)
    here = lax.broadcasted_iota(jnp.int32, shape, 0) == lax.broadcasted_iota(jnp.int32, shape, 1)
    rider = jnp.sum(jnp.where(here, squares, 0.0), axis=0, keepdims=True)
    for peer in range(peers):
        out_ref[pl.ds(peer * stride + stride - 1, 1), :] = rider


def riders_body(peers, stride, copies, arrived_ref, out_ref):
    total = arrived_ref[pl.ds(stride - 1, 1), :]
    for peer in range(1, peers):
        total = total + arrived_ref[pl.ds(peer * stride + stride - 1, 1), :]
    out_ref[...] = jnp.broadcast_to(total, (copies, HS))


def owned_body(peers, per_peer, rows, arrived_ref, out_ref):
    stride = per_peer * rows + 1
    for peer in range(peers):
        for nth in range(per_peer):
            out_ref[nth, peer] = arrived_ref[pl.ds(peer * stride + nth * rows, rows), :]


def per_device(partial_grads, joined_block, head_slot):
    own_rows = partial_grads[0]
    blocks = joined_block.shape[0]
    groups = lax.axis_size(GRP)
    width = own_rows.shape[1]
    rows = own_rows.shape[0] // groups
    peers = lax.axis_size(SHARD)
    per_peer = (blocks + peers - 1) // peers
    slot_total = per_peer * peers
    first_slot = lax.axis_index(SHARD) * per_peer
    stride = per_peer * rows + 1

    block_ids = jnp.arange(blocks, dtype=jnp.int32)
    slot_ids = jnp.arange(slot_total, dtype=jnp.int32)
    matches = (head_slot[None, :] == slot_ids[:, None]).astype(jnp.int32)
    occupied = jnp.sum(matches, axis=1)
    source = jnp.sum(matches * joined_block[None, :], axis=1)
    block_kind = (block_ids >= QH).astype(jnp.int32) + (block_ids >= QH + KVH).astype(jnp.int32)
    slot_kind = jnp.sum(matches * block_kind[None, :], axis=1) + (1 - occupied) * 3
    own = slot_ids[None, :] == first_slot + jnp.arange(per_peer, dtype=jnp.int32)[:, None]
    alike = slot_kind[None, :] == jnp.arange(3, dtype=jnp.int32)[:, None]

    parts = lax.all_to_all(own_rows.reshape(groups, rows, width), GRP, 0, 0, tiled=True)
    summed = jnp.sum(parts.astype(jnp.float32), axis=0)

    outgoing = pl.pallas_call(
        functools.partial(outgoing_body, peers, per_peer),
        out_shape=jax.ShapeDtypeStruct((peers * stride, HS), jnp.float32),
        in_specs=[IN_SMEM, IN_SMEM, IN_VMEM],
        out_specs=IN_VMEM,
        compiler_params=PARAMS,
    )(source, occupied, summed)
    arrived = lax.all_to_all(outgoing[:, None], SHARD, split_axis=0, concat_axis=0, tiled=True)
    arrived = arrived[:, 0]
    riders = pl.pallas_call(
        functools.partial(riders_body, peers, stride, groups),
        out_shape=jax.ShapeDtypeStruct((groups, HS), jnp.float32),
        in_specs=[IN_VMEM],
        out_specs=IN_VMEM,
        compiler_params=PARAMS,
    )(arrived)
    every = lax.all_to_all(riders[:, None], GRP, split_axis=0, concat_axis=0, tiled=True)
    owned_block = pl.pallas_call(
        functools.partial(owned_body, peers, per_peer, rows),
        out_shape=jax.ShapeDtypeStruct((per_peer, peers, rows, HS), jnp.float32),
        in_specs=[IN_VMEM],
        out_specs=IN_VMEM,
        compiler_params=PARAMS,
        cost_estimate=pl.CostEstimate(flops=10**6, bytes_accessed=2**19, transcendentals=0),
    )(arrived)

    every_square = every.sum(axis=(0, 1))[:slot_total]
    wanted = jnp.concatenate([own, alike], axis=0).astype(jnp.float32)
    sums = jnp.sum(wanted * every_square[None, :], axis=1)
    head_rms = jnp.sqrt(sums[:per_peer] / (D * HS))
    counts = jnp.array([QH, KVH, KVH], jnp.float32) * (D * HS)
    type_rms = jnp.sqrt(sums[per_peer:] / counts)
    return (owned_block, head_rms, type_rms)


def solution(mesh):
    finer = Mesh(mesh.devices.reshape(8, 2, 4, 8), ("grp_0", "grp_1", "shard_0", "shard_1"))
    in_specs = (P(GRP, SHARD, None), P(), P())
    out_specs = (P(SHARD, None, GRP, None), P(SHARD), P())
    return jax.shard_map(
        per_device, mesh=finer, in_specs=in_specs, out_specs=out_specs, check_vma=False
    )
```

time: 91.2 us -> 89.2 us (0.978)
  the two profiles are of different devices: /device:TPU:8 before, /device:TPU:1 now
where the time goes in v2:
time: 89.2 us; the launch traced here: 88.9 us
  waiting for transfers between devices  56.3 us (63%)
  starting transfers between devices  27.3 us (31%)
  Pallas kernels  2.85 us (3%)
  other arithmetic  1.69 us (2%)
    all_to_all x1, waiting for transfers between devices, per_device(): lax.all_to_all(own_rows.reshape(groups, rows, width), GRP, 0, 0, tiled=True)  38.4 us
    all_to_all x1, starting transfers between devices, per_device(): lax.all_to_all(own_rows.reshape(groups, rows, width), GRP, 0, 0, tiled=True)  12 us
    all_to_all x1, waiting for transfers between devices, per_device(): lax.all_to_all(outgoing[:, None], SHARD, split_axis=0, concat_axis=0, til...  11.7 us
    all_to_all x1, starting transfers between devices, per_device(): lax.all_to_all(outgoing[:, None], SHARD, split_axis=0, concat_axis=0, til...  9.67 us
    all_to_all x1, waiting for transfers between devices, per_device(): lax.all_to_all(riders[:, None], GRP, split_axis=0, concat_axis=0, tiled=T...  6.26 us
    all_to_all x1, starting transfers between devices, per_device(): lax.all_to_all(riders[:, None], GRP, split_axis=0, concat_axis=0, tiled=T...  5.7 us
  transfers between devices with their start and end apart: 3, of which 3 were waited for; matrix products, arithmetic and copies ran while one was open for 0% of the time, Pallas kernels for 1%

profile of v2, /device:TPU:1, one launch (start us, length us, event | category | flops | bytes accessed | tf_op | source)
XLA Modules:
  0.0 88.9 jit_solution(6869594621998655890)
XLA Ops:
  0.6 0.0 copy-start
  0.6 0.0 copy-start.1
  0.7 12.0 %all-to-all-start = ((bf16[16,8,6144]{2,1,0:T(8,128)(2,1)}), bf16[16,8,6144]{2,1,0:T(8,128)(2,1)S(1)}, u32[]{:S(2)}, u32[]{:S(2)}) async-start(bf16[16,8,6144]{2,1,0:T(8,128)(2,1)} %bitcast.11), calls=%async_computation | async-start | bytes 3145728 | tf_op jit(solution)/shard_map/all_to_all | solution.py:77
  12.6 0.0 copy-done
  12.6 0.0 copy-done.1
  12.6 0.1 select_reduce_fusion
  12.7 0.0 copy-start.2
  12.8 38.4 %all-to-all-done = bf16[16,8,6144]{2,1,0:T(8,128)(2,1)S(1)} async-done(((bf16[16,8,6144]{2,1,0:T(8,128)(2,1)}), bf16[16,8,6144]{2,1,0:T(8,128)(2,1)S(1)}, u32[]{:S(2)}, u32[]{:S(2)}) %all-to-all-start) | async-done | bytes 1572896 | tf_op jit(solution)/shard_map/all_to_all | solution.py:77
  51.1 0.2 convert_reduce_fusion.summed_ref
  51.4 1.5 %shard_map.67 = f32[544,128]{1,0:T(8,128)} custom-call(s32[64]{0:T(128)S(1)} %get-tuple-element.5.source_ref, s32[64]{0:T(128)S(1)} %get-tuple-element.4.occupied_ref, f32[8,6144]{1,0:T(8,128)S(1)} %convert_reduce_fusion.summed_ref), custom_call_target="tpu_custom_call" | custom-call | tf_op jit(solution)/shard_map/pallas_call | solution.py:80
  52.9 9.7 %all-to-all-start.1 = ((f32[544,1,128]{2,1,0:T(1,128)}), f32[544,1,128]{2,1,0:T(1,128)S(1)}, u32[]{:S(2)}, u32[]{:S(2)}) async-start(f32[544,1,128]{2,1,0:T(1,128)} %bitcast.2), calls=%async_computation.1 | async-start | bytes 557056 | tf_op jit(solution)/shard_map/all_to_all | solution.py:87
  62.6 11.7 %all-to-all-done.1 = f32[544,1,128]{2,1,0:T(1,128)S(1)} async-done(((f32[544,1,128]{2,1,0:T(1,128)}), f32[544,1,128]{2,1,0:T(1,128)S(1)}, u32[]{:S(2)}, u32[]{:S(2)}) %all-to-all-start.1) | async-done | bytes 278560 | tf_op jit(solution)/shard_map/all_to_all | solution.py:87
  74.2 0.6 shard_map.69
  74.9 5.7 %all-to-all-start.2 = ((f32[16,1,128]{2,1,0:T(1,128)}), f32[16,1,128]{2,1,0:T(1,128)S(1)}, u32[]{:S(2)}, u32[]{:S(2)}) async-start(f32[16,1,128]{2,1,0:T(1,128)} %bitcast.5), calls=%async_computation.2 | async-start | bytes 16384 | tf_op jit(solution)/shard_map/all_to_all | solution.py:96
  80.6 0.1 iota_compare_fusion.2
  80.6 0.7 shard_map.68
  81.4 6.3 %all-to-all-done.2 = f32[16,1,128]{2,1,0:T(1,128)S(1)} async-done(((f32[16,1,128]{2,1,0:T(1,128)}), f32[16,1,128]{2,1,0:T(1,128)S(1)}, u32[]{:S(2)}, u32[]{:S(2)}) %all-to-all-start.2) | async-done | bytes 8224 | tf_op jit(solution)/shard_map/all_to_all | solution.py:96
  87.7 0.1 select_reduce_fusion.2
  87.8 0.5 multiply_sqrt_fusion.1
  88.3 0.0 copy-done.2
  88.3 0.6 multiply_sqrt_fusion
  (5 shorter events, 0.1 us)
Async XLA Ops:
  0.6 12.0 %copy-start = (s32[48]{0:T(128)S(1)}, s32[48]{0:T(128)}, u32[]{:S(2)}) copy-start(s32[48]{0:T(128)} %param.6) | copy-start | bytes 580
  0.6 12.0 %copy-start.1 = (s32[48]{0:T(128)S(1)}, s32[48]{0:T(128)}, u32[]{:S(2)}) copy-start(s32[48]{0:T(128)} %param.5) | copy-start | bytes 580
  0.7 50.5 %all-to-all-start = ((bf16[16,8,6144]{2,1,0:T(8,128)(2,1)}), bf16[16,8,6144]{2,1,0:T(8,128)(2,1)S(1)}, u32[]{:S(2)}, u32[]{:S(2)}) async-start(bf16[16,8,6144]{2,1,0:T(8,128)(2,1)} %bitcast.11), calls=%async_computation | async-start | bytes 3145728 | tf_op jit(solution)/shard_map/all_to_all | solution.py:77
  12.7 75.6 %copy-start.2 = (f32[3]{0:T(128)S(1)}, f32[3]{0:T(128)}, u32[]{:S(2)}) copy-start(f32[3]{0:T(128)} %constant.37) | copy-start | bytes 40
  52.9 21.4 %all-to-all-start.1 = ((f32[544,1,128]{2,1,0:T(1,128)}), f32[544,1,128]{2,1,0:T(1,128)S(1)}, u32[]{:S(2)}, u32[]{:S(2)}) async-start(f32[544,1,128]{2,1,0:T(1,128)} %bitcast.2), calls=%async_computation.1 | async-start | bytes 557056 | tf_op jit(solution)/shard_map/all_to_all | solution.py:87
  74.9 12.8 %all-to-all-start.2 = ((f32[16,1,128]{2,1,0:T(1,128)}), f32[16,1,128]{2,1,0:T(1,128)S(1)}, u32[]{:S(2)}, u32[]{:S(2)}) async-start(f32[16,1,128]{2,1,0:T(1,128)} %bitcast.5), calls=%async_computation.2 | async-start | bytes 16384 | tf_op jit(solution)/shard_map/all_to_all | solution.py:96

commit v3 on v2

v3 whole, which is shorter than its diff:
```python
import functools

import jax
import jax.numpy as jnp
from jax import lax
from jax.experimental import pallas as pl
from jax.experimental.pallas import tpu as pltpu
from jax.sharding import Mesh
from jax.sharding import PartitionSpec as P

D = 4096
QH = 32
KVH = 8
HS = 128
SHARD = ("shard_0", "shard_1")
GRP = ("grp_0", "grp_1")
IN_VMEM = pl.BlockSpec(memory_space=pltpu.VMEM)
PARAMS = pltpu.CompilerParams(vmem_limit_bytes=4 * 2**20)
IN_SMEM = pl.BlockSpec(memory_space=pltpu.SMEM)


def diagonal_row(rows):
    sums = jnp.sum(rows, axis=1, keepdims=True)
    shape = rows.shape
    here = lax.broadcasted_iota(jnp.int32, shape, 0) == lax.broadcasted_iota(jnp.int32, shape, 1)
    return jnp.sum(jnp.where(here, sums, 0.0), axis=0, keepdims=True)


def squares_body(blocks, summed_ref, out_ref):
    block_rows = []
    for block in range(blocks):
        tile = summed_ref[:, pl.ds(block * HS, HS)]
        block_rows.append(jnp.sum(tile * tile, axis=0, keepdims=True))
    out_ref[...] = jnp.broadcast_to(diagonal_row(jnp.concatenate(block_rows, axis=0)), out_ref.shape)


def outgoing_body(peers, per_peer, source_ref, occupied_ref, summed_ref, squares_ref, out_ref):
    rows = summed_ref.shape[0]
    stride = per_peer * rows + 1
    rider = jnp.sum(squares_ref[...], axis=0, keepdims=True)
    for slot in range(peers * per_peer):
        first = pl.multiple_of(source_ref[slot] * HS, HS)
        tile = summed_ref[:, pl.ds(first, HS)]
        tile = jnp.where(occupied_ref[slot] > 0, tile, jnp.zeros_like(tile))
        peer, nth = divmod(slot, per_peer)
        out_ref[pl.ds(peer * stride + nth * rows, rows), :] = tile
    for peer in range(peers):
        out_ref[pl.ds(peer * stride + stride - 1, 1), :] = rider


def arrived_body(peers, per_peer, rows, arrived_ref, wanted_ref, owned_ref, head_ref, type_ref):
    stride = per_peer * rows + 1
    total = arrived_ref[pl.ds(stride - 1, 1), :]
    for peer in range(1, peers):
        total = total + arrived_ref[pl.ds(peer * stride + stride - 1, 1), :]
    sums = jnp.sum(wanted_ref[...] * total, axis=1, keepdims=True)
    row = lax.broadcasted_iota(jnp.int32, sums.shape, 0)
    heads = jnp.where(row < per_peer, 1, jnp.where(row == per_peer, QH, KVH))
    rms = jnp.sqrt(sums / (heads.astype(jnp.float32) * (D * HS)))
    for nth in range(per_peer):
        head_ref[nth] = jnp.sum(jnp.where(row == nth, rms, 0.0))
    for kind in range(3):
        type_ref[kind] = jnp.sum(jnp.where(row == per_peer + kind, rms, 0.0))
    for peer in range(peers):
        for nth in range(per_peer):
            owned_ref[nth, peer] = arrived_ref[pl.ds(peer * stride + nth * rows, rows), :]


def per_device(partial_grads, joined_block, head_slot):
    own_rows = partial_grads[0]
    blocks = joined_block.shape[0]
    groups = lax.axis_size(GRP)
    width = own_rows.shape[1]
    rows = own_rows.shape[0] // groups
    peers = lax.axis_size(SHARD)
    per_peer = (blocks + peers - 1) // peers
    slot_total = per_peer * peers
    first_slot = lax.axis_index(SHARD) * per_peer
    stride = per_peer * rows + 1

    block_ids = jnp.arange(blocks, dtype=jnp.int32)
    slot_ids = jnp.arange(slot_total, dtype=jnp.int32)
    matches = (head_slot[None, :] == slot_ids[:, None]).astype(jnp.int32)
    occupied = jnp.sum(matches, axis=1)
    source = jnp.sum(matches * joined_block[None, :], axis=1)
    block_kind = (block_ids >= QH).astype(jnp.int32) + (block_ids >= QH + KVH).astype(jnp.int32)
    own = head_slot[None, :] == first_slot + jnp.arange(per_peer, dtype=jnp.int32)[:, None]
    alike = block_kind[None, :] == jnp.arange(3, dtype=jnp.int32)[:, None]
    asked = jnp.concatenate([own, alike], axis=0)
    joined = joined_block[:, None] == block_ids[None, :]
    wanted = jnp.any(asked[:, :, None] & joined[None], axis=1).astype(jnp.float32)
    wanted = jnp.pad(wanted, ((0, 8 - wanted.shape[0]), (0, HS - blocks)))

    parts = lax.all_to_all(own_rows.reshape(groups, rows, width), GRP, 0, 0, tiled=True)
    summed = jnp.sum(parts.astype(jnp.float32), axis=0)

    squares = pl.pallas_call(
        functools.partial(squares_body, blocks),
        out_shape=jax.ShapeDtypeStruct((groups, HS), jnp.float32),
        in_specs=[IN_VMEM],
        out_specs=IN_VMEM,
        compiler_params=PARAMS,
    )(summed)
    squares = lax.all_to_all(squares[:, None], GRP, split_axis=0, concat_axis=0, tiled=True)[:, 0]
    outgoing = pl.pallas_call(
        functools.partial(outgoing_body, peers, per_peer),
        out_shape=jax.ShapeDtypeStruct((peers * stride, HS), jnp.float32),
        in_specs=[IN_SMEM, IN_SMEM, IN_VMEM, IN_VMEM],
        out_specs=IN_VMEM,
        compiler_params=PARAMS,
    )(source, occupied, summed, squares)
    arrived = lax.all_to_all(outgoing[:, None], SHARD, split_axis=0, concat_axis=0, tiled=True)
    return pl.pallas_call(
        functools.partial(arrived_body, peers, per_peer, rows),
        out_shape=(
            jax.ShapeDtypeStruct((per_peer, peers, rows, HS), jnp.float32),
            jax.ShapeDtypeStruct((per_peer,), jnp.float32),
            jax.ShapeDtypeStruct((3,), jnp.float32),
        ),
        in_specs=[IN_VMEM, IN_VMEM],
        out_specs=(IN_VMEM, IN_SMEM, IN_SMEM),
        compiler_params=PARAMS,
    )(arrived[:, 0], wanted)


def solution(mesh):
    finer = Mesh(mesh.devices.reshape(8, 2, 4, 8), ("grp_0", "grp_1", "shard_0", "shard_1"))
    in_specs = (P(GRP, SHARD, None), P(), P())
    out_specs = (P(SHARD, None, GRP, None), P(SHARD), P())
    return jax.shard_map(
        per_device, mesh=finer, in_specs=in_specs, out_specs=out_specs, check_vma=False
    )
```

time: 89.2 us -> 87.6 us (0.982)
  the two profiles are of different devices: /device:TPU:1 before, /device:TPU:8 now
where the time goes in v3:
time: 87.6 us; the launch traced here: 87.3 us
  waiting for transfers between devices  57.5 us (66%)
  starting transfers between devices  25.4 us (29%)
  Pallas kernels  2.97 us (3%)
    all_to_all x1, waiting for transfers between devices, per_device(): lax.all_to_all(own_rows.reshape(groups, rows, width), GRP, 0, 0, tiled=True)  37.7 us
    all_to_all x1, waiting for transfers between devices, per_device(): lax.all_to_all(outgoing[:, None], SHARD, split_axis=0, concat_axis=0, til...  12.4 us
    all_to_all x1, starting transfers between devices, per_device(): lax.all_to_all(own_rows.reshape(groups, rows, width), GRP, 0, 0, tiled=True)  10.4 us
    all_to_all x1, starting transfers between devices, per_device(): lax.all_to_all(outgoing[:, None], SHARD, split_axis=0, concat_axis=0, til...  10.2 us
    all_to_all x1, waiting for transfers between devices, per_device(): lax.all_to_all(squares[:, None], GRP, split_axis=0, concat_axis=0, tiled=...  7.42 us
    all_to_all x1, starting transfers between devices, per_device(): lax.all_to_all(squares[:, None], GRP, split_axis=0, concat_axis=0, tiled=...  4.8 us
  transfers between devices with their start and end apart: 3, of which 3 were waited for; matrix products, arithmetic and copies ran while one was open for 0% of the time, Pallas kernels for 0%

profile of v3, /device:TPU:8, one launch (start us, length us, event | category | flops | bytes accessed | tf_op | source)
XLA Modules:
  0.0 87.3 jit_solution(1738724266581649913)
XLA Ops:
  0.6 0.0 copy-start.1
  0.6 10.4 %all-to-all-start = ((bf16[16,8,6144]{2,1,0:T(8,128)(2,1)}), bf16[16,8,6144]{2,1,0:T(8,128)(2,1)S(1)}, u32[]{:S(2)}, u32[]{:S(2)}) async-start(bf16[16,8,6144]{2,1,0:T(8,128)(2,1)} %bitcast.11), calls=%async_computation | async-start | bytes 3145728 | tf_op jit(solution)/shard_map/all_to_all | solution.py:94
  11.1 0.0 copy-start
  11.1 0.0 copy-done.1
  11.1 0.1 broadcast_compare_fusion
  11.2 37.7 %all-to-all-done = bf16[16,8,6144]{2,1,0:T(8,128)(2,1)S(1)} async-done(((bf16[16,8,6144]{2,1,0:T(8,128)(2,1)}), bf16[16,8,6144]{2,1,0:T(8,128)(2,1)S(1)}, u32[]{:S(2)}, u32[]{:S(2)}) %all-to-all-start) | async-done | bytes 1572896 | tf_op jit(solution)/shard_map/all_to_all | solution.py:94
  48.9 0.2 convert_reduce_fusion.summed_ref
  49.2 0.7 shard_map.58
  49.9 4.8 %all-to-all-start.1 = ((f32[16,1,128]{2,1,0:T(1,128)}), f32[16,1,128]{2,1,0:T(1,128)S(1)}, u32[]{:S(2)}, u32[]{:S(2)}) async-start(f32[16,1,128]{2,1,0:T(1,128)} %bitcast.2), calls=%async_computation.1 | async-start | bytes 16384 | tf_op jit(solution)/shard_map/all_to_all | solution.py:104
  54.7 0.0 copy-done
  54.7 0.1 convert_reduce_fusion.1
  54.8 7.4 %all-to-all-done.1 = f32[16,1,128]{2,1,0:T(1,128)S(1)} async-done(((f32[16,1,128]{2,1,0:T(1,128)}), f32[16,1,128]{2,1,0:T(1,128)S(1)}, u32[]{:S(2)}, u32[]{:S(2)}) %all-to-all-start.1) | async-done | bytes 8224 | tf_op jit(solution)/shard_map/all_to_all | solution.py:104
  62.2 1.4 %shard_map.59 = f32[544,128]{1,0:T(8,128)} custom-call(s32[64]{0:T(128)S(1)} %get-tuple-element.4.source_ref, s32[64]{0:T(128)S(1)} %get-tuple-element.3.occupied_ref, f32[8,6144]{1,0:T(8,128)S(1)} %convert_reduce_fusion.summed_ref, f32[16,128]{1,0:T(8,128)S(1)} %bitcast.10), custom_call_target="tpu_custom_call" | custom-call | tf_op jit(solution)/shard_map/pallas_call | solution.py:105
  63.6 10.2 %all-to-all-start.2 = ((f32[544,1,128]{2,1,0:T(1,128)}), f32[544,1,128]{2,1,0:T(1,128)S(1)}, u32[]{:S(2)}, u32[]{:S(2)}) async-start(f32[544,1,128]{2,1,0:T(1,128)} %bitcast.5), calls=%async_computation.2 | async-start | bytes 557056 | tf_op jit(solution)/shard_map/all_to_all | solution.py:112
  73.8 0.1 iota_compare_fusion
  73.9 0.1 and_reduce_fusion
  74.0 12.4 %all-to-all-done.2 = f32[544,1,128]{2,1,0:T(1,128)S(1)} async-done(((f32[544,1,128]{2,1,0:T(1,128)}), f32[544,1,128]{2,1,0:T(1,128)S(1)}, u32[]{:S(2)}, u32[]{:S(2)}) %all-to-all-start.2) | async-done | bytes 278560 | tf_op jit(solution)/shard_map/all_to_all | solution.py:112
  86.4 0.8 shard_map.60
  (5 shorter events, 0.0 us)
Async XLA Ops:
  0.6 10.5 %copy-start.1 = (s32[48]{0:T(128)S(1)}, s32[48]{0:T(128)}, u32[]{:S(2)}) copy-start(s32[48]{0:T(128)} %param.5) | copy-start | bytes 580
  0.6 48.3 %all-to-all-start = ((bf16[16,8,6144]{2,1,0:T(8,128)(2,1)}), bf16[16,8,6144]{2,1,0:T(8,128)(2,1)S(1)}, u32[]{:S(2)}, u32[]{:S(2)}) async-start(bf16[16,8,6144]{2,1,0:T(8,128)(2,1)} %bitcast.11), calls=%async_computation | async-start | bytes 3145728 | tf_op jit(solution)/shard_map/all_to_all | solution.py:94
  11.1 43.6 %copy-start = (s32[48]{0:T(128)S(1)}, s32[48]{0:T(128)}, u32[]{:S(2)}) copy-start(s32[48]{0:T(128)} %param.4) | copy-start | bytes 580
  49.9 12.3 %all-to-all-start.1 = ((f32[16,1,128]{2,1,0:T(1,128)}), f32[16,1,128]{2,1,0:T(1,128)S(1)}, u32[]{:S(2)}, u32[]{:S(2)}) async-start(f32[16,1,128]{2,1,0:T(1,128)} %bitcast.2), calls=%async_computation.1 | async-start | bytes 16384 | tf_op jit(solution)/shard_map/all_to_all | solution.py:104
  63.6 22.8 %all-to-all-start.2 = ((f32[544,1,128]{2,1,0:T(1,128)}), f32[544,1,128]{2,1,0:T(1,128)S(1)}, u32[]{:S(2)}, u32[]{:S(2)}) async-start(f32[544,1,128]{2,1,0:T(1,128)} %bitcast.5), calls=%async_computation.2 | async-start | bytes 557056 | tf_op jit(solution)/shard_map/all_to_all | solution.py:112

commit v4 on v3

--- a/solution.py
+++ b/solution.py
@@ -14,6 +14,7 @@
 HS = 128
 SHARD = ("shard_0", "shard_1")
 GRP = ("grp_0", "grp_1")
+SCALES = 64
 IN_VMEM = pl.BlockSpec(memory_space=pltpu.VMEM)
 PARAMS = pltpu.CompilerParams(vmem_limit_bytes=4 * 2**20)
 IN_SMEM = pl.BlockSpec(memory_space=pltpu.SMEM)
@@ -34,36 +35,90 @@
     out_ref[...] = jnp.broadcast_to(diagonal_row(jnp.concatenate(block_rows, axis=0)), out_ref.shape)
 
 
-def outgoing_body(peers, per_peer, source_ref, occupied_ref, summed_ref, squares_ref, out_ref):
+def halves(exponent):
+    return jnp.exp2(exponent * 0.5)
+
+
+def words_of(values):
+    exponent = jnp.floor(jnp.log2(jnp.maximum(values, 1e-37)))
+    down = halves(-exponent)
+    mantissa = jnp.floor(values * down * down * 2.0**18).astype(jnp.int32) + 1
+    return jnp.where(values > 0.0, mantissa * 1024 + exponent.astype(jnp.int32) + 512, 0), exponent
+
+
+def mantissa_of(words):
+    return (words >> 10).astype(jnp.float32) * 2.0**-18
+
+
+def exponent_of(words):
+    return ((words & 1023) - 512).astype(jnp.float32)
+
+
+def code_tile(tile, first_lane):
+    most = jnp.max(jnp.abs(tile), axis=1, keepdims=True)
+    words, exponent = words_of(most)
+    down = halves(-exponent)
+    gain = 32767.0 / jnp.where(words > 0, mantissa_of(words), 1.0)
+    codes = jnp.floor(tile * down * down * gain + 0.5).astype(jnp.int32)
+    row = lax.broadcasted_iota(jnp.int32, tile.shape, 0)
+    lane = lax.broadcasted_iota(jnp.int32, tile.shape, 1)
+    return codes, jnp.sum(jnp.where(lane == row + first_lane, words, 0), axis=0, keepdims=True)
+
+
+def packed_body(peers, source_ref, occupied_ref, summed_ref, out_ref):
     rows = summed_ref.shape[0]
-    stride = per_peer * rows + 1
-    rider = jnp.sum(squares_ref[...], axis=0, keepdims=True)
-    for slot in range(peers * per_peer):
+
+    def coded(slot, first_lane):
         first = pl.multiple_of(source_ref[slot] * HS, HS)
         tile = summed_ref[:, pl.ds(first, HS)]
-        tile = jnp.where(occupied_ref[slot] > 0, tile, jnp.zeros_like(tile))
-        peer, nth = divmod(slot, per_peer)
-        out_ref[pl.ds(peer * stride + nth * rows, rows), :] = tile
+        return code_tile(jnp.where(occupied_ref[slot] > 0, tile, jnp.zeros_like(tile)), first_lane)
+
     for peer in range(peers):
-        out_ref[pl.ds(peer * stride + stride - 1, 1), :] = rider
+        high, high_words = coded(2 * peer, SCALES)
+        low, low_words = coded(2 * peer + 1, SCALES + rows)
+        start = peer * (rows + 1)
+        out_ref[pl.ds(start, rows), :] = (high << 16) | (low & 65535)
+        out_ref[pl.ds(start + rows, 1), :] = high_words + low_words
 
 
-def arrived_body(peers, per_peer, rows, arrived_ref, wanted_ref, owned_ref, head_ref, type_ref):
-    stride = per_peer * rows + 1
-    total = arrived_ref[pl.ds(stride - 1, 1), :]
-    for peer in range(1, peers):
-        total = total + arrived_ref[pl.ds(peer * stride + stride - 1, 1), :]
+def outgoing_body(peers, rows, packed_ref, squares_ref, out_ref):
+    words, _ = words_of(jnp.sum(squares_ref[...], axis=0, keepdims=True))
+    for peer in range(peers):
+        start = peer * (rows + 1)
+        out_ref[pl.ds(start, rows), :] = packed_ref[pl.ds(start, rows), :]
+        out_ref[pl.ds(start + rows, 1), :] = packed_ref[pl.ds(start + rows, 1), :] + words
+
+
+def arrived_body(peers, rows, blocks, arrived_ref, wanted_ref, owned_ref, head_ref, type_ref):
+    riders = [arrived_ref[pl.ds(peer * (rows + 1) + rows, 1), :] for peer in range(peers)]
+    riders = jnp.concatenate(riders, axis=0)
+    mantissa = mantissa_of(riders)
+    up = halves(exponent_of(riders))
+    lanes = lax.broadcasted_iota(jnp.int32, riders.shape, 1)
+    total = jnp.sum(jnp.where(lanes < blocks, mantissa * up * up, 0.0), axis=0, keepdims=True)
     sums = jnp.sum(wanted_ref[...] * total, axis=1, keepdims=True)
-    row = lax.broadcasted_iota(jnp.int32, sums.shape, 0)
-    heads = jnp.where(row < per_peer, 1, jnp.where(row == per_peer, QH, KVH))
+    at = lax.broadcasted_iota(jnp.int32, sums.shape, 0)
+    heads = jnp.where(at < 2, 1, jnp.where(at == 2, QH, KVH))
     rms = jnp.sqrt(sums / (heads.astype(jnp.float32) * (D * HS)))
-    for nth in range(per_peer):
-        head_ref[nth] = jnp.sum(jnp.where(row == nth, rms, 0.0))
+    for nth in range(2):
+        head_ref[nth] = jnp.sum(jnp.where(at == nth, rms, 0.0))
     for kind in range(3):
-        type_ref[kind] = jnp.sum(jnp.where(row == per_peer + kind, rms, 0.0))
+        type_ref[kind] = jnp.sum(jnp.where(at == 2 + kind, rms, 0.0))
+
+    step = mantissa * up * (1.0 / 32767.0)
+    row = lax.broadcasted_iota(jnp.int32, (rows, HS), 0)
+    lane = lax.broadcasted_iota(jnp.int32, (rows, HS), 1)
+
+    def column(values, peer, nth):
+        spread = jnp.broadcast_to(values[peer : peer + 1], (rows, HS))
+        picked = jnp.where(lane == row + (SCALES + nth * rows), spread, 0.0)
+        return jnp.sum(picked, axis=1, keepdims=True)
+
     for peer in range(peers):
-        for nth in range(per_peer):
-            owned_ref[nth, peer] = arrived_ref[pl.ds(peer * stride + nth * rows, rows), :]
+        codes = arrived_ref[pl.ds(peer * (rows + 1), rows), :]
+        for nth, code in enumerate((codes >> 16, (codes << 16) >> 16)):
+            value = code.astype(jnp.float32) * column(step, peer, nth) * column(up, peer, nth)
+            owned_ref[nth, peer] = value
 
 
 def per_device(partial_grads, joined_block, head_slot):
@@ -76,7 +131,6 @@
     per_peer = (blocks + peers - 1) // peers
     slot_total = per_peer * peers
     first_slot = lax.axis_index(SHARD) * per_peer
-    stride = per_peer * rows + 1
 
     block_ids = jnp.arange(blocks, dtype=jnp.int32)
     slot_ids = jnp.arange(slot_total, dtype=jnp.int32)
@@ -102,16 +156,25 @@
         compiler_params=PARAMS,
     )(summed)
     squares = lax.all_to_all(squares[:, None], GRP, split_axis=0, concat_axis=0, tiled=True)[:, 0]
-    outgoing = pl.pallas_call(
-        functools.partial(outgoing_body, peers, per_peer),
-        out_shape=jax.ShapeDtypeStruct((peers * stride, HS), jnp.float32),
-        in_specs=[IN_SMEM, IN_SMEM, IN_VMEM, IN_VMEM],
+    packed_shape = jax.ShapeDtypeStruct((peers * (rows + 1), HS), jnp.int32)
+    packed = pl.pallas_call(
+        functools.partial(packed_body, peers),
+        out_shape=packed_shape,
+        in_specs=[IN_SMEM, IN_SMEM, IN_VMEM],
         out_specs=IN_VMEM,
         compiler_params=PARAMS,
-    )(source, occupied, summed, squares)
+        cost_estimate=pl.CostEstimate(flops=4 * 10**6, bytes_accessed=2**19, transcendentals=0),
+    )(source, occupied, summed)
+    outgoing = pl.pallas_call(
+        functools.partial(outgoing_body, peers, rows),
+        out_shape=packed_shape,
+        in_specs=[IN_VMEM, IN_VMEM],
+        out_specs=IN_VMEM,
+        compiler_params=PARAMS,
+    )(packed, squares)
     arrived = lax.all_to_all(outgoing[:, None], SHARD, split_axis=0, concat_axis=0, tiled=True)
     return pl.pallas_call(
-        functools.partial(arrived_body, peers, per_peer, rows),
+        functools.partial(arrived_body, peers, rows, blocks),
         out_shape=(
             jax.ShapeDtypeStruct((per_peer, peers, rows, HS), jnp.float32),
             jax.ShapeDtypeStruct((per_peer,), jnp.float32),

time: 87.6 us -> 84.5 us (0.965)
  waiting for transfers between devices: 57.5 us -> 53.9 us
    all_to_all x1, waiting for transfers between devices: 12.4 us -> 9.9 us  [per_device(): lax.all_to_all(outgoing[:, None], SHARD, split_axis=0, concat_axis=0, til...]
    all_to_all x1, waiting for transfers between devices: 7.42 us -> 6.37 us  [per_device(): lax.all_to_all(squares[:, None], GRP, split_axis=0, concat_axis=0, tiled=...]
    pallas_call x2 -> x3, Pallas kernels: 2.24 us -> 2.72 us  [the longest x1 1.05 us: per_device(): pl.pallas_call(functools.partial(packed_body, peers), out_shape=packed_sh...]
  transfers between devices with their start and end apart: 3 -> 3, of which waited for: 3 -> 3; matrix products, arithmetic and copies ran while one was open for 0% -> 0% of each run, Pallas kernels for 0% -> 1%
where the time goes in v4:
time: 84.5 us; the launch traced here: 84.3 us
  waiting for transfers between devices  53.9 us (64%)
  starting transfers between devices  25.5 us (30%)
  Pallas kernels  3.46 us (4%)
    all_to_all x1, waiting for transfers between devices, per_device(): lax.all_to_all(own_rows.reshape(groups, rows, width), GRP, 0, 0, tiled=True)  37.7 us
    all_to_all x1, starting transfers between devices, per_device(): lax.all_to_all(own_rows.reshape(groups, rows, width), GRP, 0, 0, tiled=True)  10.6 us
    all_to_all x1, starting transfers between devices, per_device(): lax.all_to_all(outgoing[:, None], SHARD, split_axis=0, concat_axis=0, til...  10.2 us
    all_to_all x1, waiting for transfers between devices, per_device(): lax.all_to_all(outgoing[:, None], SHARD, split_axis=0, concat_axis=0, til...  9.9 us
    all_to_all x1, waiting for transfers between devices, per_device(): lax.all_to_all(squares[:, None], GRP, split_axis=0, concat_axis=0, tiled=...  6.37 us
    all_to_all x1, starting transfers between devices, per_device(): lax.all_to_all(squares[:, None], GRP, split_axis=0, concat_axis=0, tiled=...  4.8 us
  transfers between devices with their start and end apart: 3, of which 3 were waited for; matrix products, arithmetic and copies ran while one was open for 0% of the time, Pallas kernels for 1%

profile of v4, /device:TPU:8, one launch (start us, length us, event | category | flops | bytes accessed | tf_op | source)
XLA Modules:
  0.0 84.3 jit_solution(616405112655078995)
XLA Ops:
  0.6 0.0 copy-start.1
  0.6 0.0 copy-start
  0.7 10.6 %all-to-all-start = ((bf16[16,8,6144]{2,1,0:T(8,128)(2,1)}), bf16[16,8,6144]{2,1,0:T(8,128)(2,1)S(1)}, u32[]{:S(2)}, u32[]{:S(2)}) async-start(bf16[16,8,6144]{2,1,0:T(8,128)(2,1)} %bitcast.11), calls=%async_computation | async-start | bytes 3145728 | tf_op jit(solution)/shard_map/all_to_all | solution.py:148
  11.3 0.0 copy-done.1
  11.3 0.1 broadcast_compare_fusion
  11.3 0.0 copy-done
  11.4 0.1 iota_compare_fusion
  11.4 37.7 %all-to-all-done = bf16[16,8,6144]{2,1,0:T(8,128)(2,1)S(1)} async-done(((bf16[16,8,6144]{2,1,0:T(8,128)(2,1)}), bf16[16,8,6144]{2,1,0:T(8,128)(2,1)S(1)}, u32[]{:S(2)}, u32[]{:S(2)}) %all-to-all-start) | async-done | bytes 1572896 | tf_op jit(solution)/shard_map/all_to_all | solution.py:148
  49.1 0.2 convert_reduce_fusion.summed_ref
  49.3 0.7 shard_map.59
  50.0 4.8 %all-to-all-start.1 = ((f32[16,1,128]{2,1,0:T(1,128)}), f32[16,1,128]{2,1,0:T(1,128)S(1)}, u32[]{:S(2)}, u32[]{:S(2)}) async-start(f32[16,1,128]{2,1,0:T(1,128)} %bitcast.2), calls=%async_computation.1 | async-start | bytes 16384 | tf_op jit(solution)/shard_map/all_to_all | solution.py:158
  54.8 0.1 convert_reduce_fusion.1
  54.9 1.1 %shard_map.58.packed_ref = s32[288,128]{1,0:T(8,128)S(1)} custom-call(s32[64]{0:T(128)S(1)} %get-tuple-element.4.source_ref, s32[64]{0:T(128)S(1)} %get-tuple-element.3.occupied_ref, f32[8,6144]{1,0:T(8,128)S(1)} %convert_reduce_fusion.summed_ref), custom_call_target="tpu_custom_call" | custom-call | flops 4000000 | bytes 524288 | tf_op jit(solution)/shard_map/pallas_call | solution.py:160
  56.0 6.4 %all-to-all-done.1 = f32[16,1,128]{2,1,0:T(1,128)S(1)} async-done(((f32[16,1,128]{2,1,0:T(1,128)}), f32[16,1,128]{2,1,0:T(1,128)S(1)}, u32[]{:S(2)}, u32[]{:S(2)}) %all-to-all-start.1) | async-done | bytes 8224 | tf_op jit(solution)/shard_map/all_to_all | solution.py:158
  62.4 0.7 shard_map.60
  63.1 10.2 %all-to-all-start.2 = ((s32[288,1,128]{2,1,0:T(1,128)}), s32[288,1,128]{2,1,0:T(1,128)S(1)}, u32[]{:S(2)}, u32[]{:S(2)}) async-start(s32[288,1,128]{2,1,0:T(1,128)} %bitcast.5), calls=%async_computation.2 | async-start | bytes 294912 | tf_op jit(solution)/shard_map/all_to_all | solution.py:175
  73.3 0.1 and_reduce_fusion
  73.4 9.9 %all-to-all-done.2 = s32[288,1,128]{2,1,0:T(1,128)S(1)} async-done(((s32[288,1,128]{2,1,0:T(1,128)}), s32[288,1,128]{2,1,0:T(1,128)S(1)}, u32[]{:S(2)}, u32[]{:S(2)}) %all-to-all-start.2) | async-done | bytes 147488 | tf_op jit(solution)/shard_map/all_to_all | solution.py:175
  83.3 1.0 %shard_map.61 = (f32[2,32,8,128]{3,2,1,0:T(8,128)}, f32[2]{0:T(128)}, f32[3]{0:T(128)}) custom-call(s32[288,128]{1,0:T(8,128)S(1)} %bitcast.9, f32[8,128]{1,0:T(8,128)S(1)} %pad_convert_fusion.wanted_ref), custom_call_target="tpu_custom_call" | custom-call | tf_op jit(solution)/shard_map/pallas_call | solution.py:176
  (5 shorter events, 0.0 us)
Async XLA Ops:
  0.6 10.6 %copy-start.1 = (s32[48]{0:T(128)S(1)}, s32[48]{0:T(128)}, u32[]{:S(2)}) copy-start(s32[48]{0:T(128)} %param.5) | copy-start | bytes 580
  0.6 10.7 %copy-start = (s32[48]{0:T(128)S(1)}, s32[48]{0:T(128)}, u32[]{:S(2)}) copy-start(s32[48]{0:T(128)} %param.4) | copy-start | bytes 580
  0.7 48.4 %all-to-all-start = ((bf16[16,8,6144]{2,1,0:T(8,128)(2,1)}), bf16[16,8,6144]{2,1,0:T(8,128)(2,1)S(1)}, u32[]{:S(2)}, u32[]{:S(2)}) async-start(bf16[16,8,6144]{2,1,0:T(8,128)(2,1)} %bitcast.11), calls=%async_computation | async-start | bytes 3145728 | tf_op jit(solution)/shard_map/all_to_all | solution.py:148
  50.0 12.3 %all-to-all-start.1 = ((f32[16,1,128]{2,1,0:T(1,128)}), f32[16,1,128]{2,1,0:T(1,128)S(1)}, u32[]{:S(2)}, u32[]{:S(2)}) async-start(f32[16,1,128]{2,1,0:T(1,128)} %bitcast.2), calls=%async_computation.1 | async-start | bytes 16384 | tf_op jit(solution)/shard_map/all_to_all | solution.py:158
  63.1 20.2 %all-to-all-start.2 = ((s32[288,1,128]{2,1,0:T(1,128)}), s32[288,1,128]{2,1,0:T(1,128)S(1)}, u32[]{:S(2)}, u32[]{:S(2)}) async-start(s32[288,1,128]{2,1,0:T(1,128)} %bitcast.5), calls=%async_computation.2 | async-start | bytes 294912 | tf_op jit(solution)/shard_map/all_to_all | solution.py:175

commit v5 on v4

--- a/solution.py
+++ b/solution.py
@@ -15,8 +15,13 @@
 SHARD = ("shard_0", "shard_1")
 GRP = ("grp_0", "grp_1")
 SCALES = 64
+NOISE = 1.5e-4
+SPAN = 4
+LOWEST = 1e-18
+HIGHEST = 1e8
+LIFT = 2.0**30
 IN_VMEM = pl.BlockSpec(memory_space=pltpu.VMEM)
-PARAMS = pltpu.CompilerParams(vmem_limit_bytes=4 * 2**20)
+PARAMS = pltpu.CompilerParams(vmem_limit_bytes=8 * 2**20)
 IN_SMEM = pl.BlockSpec(memory_space=pltpu.SMEM)
 
 
@@ -52,6 +57,18 @@
 
 def exponent_of(words):
     return ((words & 1023) - 512).astype(jnp.float32)
+
+
+def count_body(peers, rows, blocks, arrived_ref, out_ref):
+    riders = [arrived_ref[pl.ds(peer * (rows + 1) + rows, 1), :] for peer in range(peers)]
+    riders = jnp.concatenate(riders, axis=0)
+    lane = lax.broadcasted_iota(jnp.int32, riders.shape, 1)
+    out_ref[0] = jnp.sum(jnp.where((lane == blocks) & (riders != 0), 1.0, 0.0))
+
+
+def value_of(words):
+    up = halves(exponent_of(words))
+    return mantissa_of(words) * up * up
 
 
 def code_tile(tile, first_lane):
@@ -121,6 +138,138 @@
             owned_ref[nth, peer] = value
 
 
+def pair_body(sums_ref, out_ref):
+    chunks, rows, width = sums_ref.shape
+    half = width // 2
+    lane = lax.broadcasted_iota(jnp.int32, (rows, HS), 1)
+
+    def chunk_step(chunk, _):
+        most = jnp.zeros((rows, HS), jnp.float32)
+        for span in range(width // (SPAN * HS)):
+            tiles = [sums_ref[chunk, :, pl.ds((SPAN * span + nth) * HS, HS)] for nth in range(SPAN)]
+            peak = functools.reduce(jnp.maximum, [jnp.abs(tile) for tile in tiles])
+            most = jnp.where(lane == span, jnp.max(peak, axis=1, keepdims=True), most)
+        words, _ = words_of(jnp.minimum(most, 2.0 * HIGHEST))
+        out_ref[chunk, :, pl.ds(half, HS)] = words
+        gain = jnp.where(words > 0, 32767.0 / jnp.maximum(value_of(words), LOWEST * 0.5), 0.0)
+        spans = width // (SPAN * HS)
+        gains = [jnp.broadcast_to(gain[:, span : span + 1], (rows, HS)) for span in range(spans)]
+        for block in range(half // HS):
+            codes = []
+            for place in (block, block + half // HS):
+                tile = sums_ref[chunk, :, pl.ds(place * HS, HS)]
+                codes.append(jnp.floor(tile * gains[place // SPAN] + 0.5).astype(jnp.int32))
+            out_ref[chunk, :, pl.ds(block * HS, HS)] = (codes[0] << 16) | (codes[1] & 65535)
+        return 0
+
+    lax.fori_loop(0, chunks, chunk_step, 0)
+
+
+def gathered_body(words_ref, summed_ref, out_ref):
+    chunks, rows, width = words_ref.shape
+    half = width - HS
+    blocks = 2 * half // HS
+    scales = [value_of(words_ref[chunk, :, pl.ds(half, HS)]) for chunk in range(chunks)]
+    lane = lax.broadcasted_iota(jnp.int32, (rows, HS), 1)
+    odd = jnp.zeros((rows, HS), jnp.float32)
+    noise = jnp.zeros((rows, HS), jnp.float32)
+    for scale in scales:
+        strange = (scale > HIGHEST) | ((scale > 0.0) & (scale < LOWEST))
+        odd = jnp.where(strange, 1.0, odd)
+        step = jnp.minimum(scale, HIGHEST) * (LIFT / 32767.0)
+        noise = noise + step * step * (HS / 12.0)
+    scales = [scale * (1.0 / 32767.0) for scale in scales]
+    noise = jnp.sum(noise, axis=0, keepdims=True)
+    noises = [jnp.where(lane[:1] // SPAN == span, noise[:, span : span + 1], 0.0) for span in range(blocks // SPAN)]
+    noise = functools.reduce(jnp.add, noises)
+    block_rows = [None] * blocks
+    for block in range(half // HS):
+        if block % SPAN == 0:
+            firsts = (block // SPAN, (block + half // HS) // SPAN)
+            steps = [
+                [jnp.broadcast_to(scale[:, span : span + 1], (rows, HS)) for span in firsts] for scale in scales
+            ]
+        totals = [jnp.zeros((rows, HS), jnp.float32)] * 2
+        for chunk in range(chunks):
+            both = words_ref[chunk, :, pl.ds(block * HS, HS)]
+            for nth, code in enumerate((both >> 16, (both << 16) >> 16)):
+                totals[nth] = totals[nth] + code.astype(jnp.float32) * steps[chunk][nth]
+        for nth, total in enumerate(totals):
+            place = block + nth * (half // HS)
+            summed_ref[:, pl.ds(place * HS, HS)] = total
+            block_rows[place] = jnp.sum(total * total, axis=0, keepdims=True)
+    squares = diagonal_row(jnp.concatenate(block_rows, axis=0))
+    odd = jnp.sum(odd, axis=0, keepdims=True)
+    bad = (noise > (LIFT * NOISE) ** 2 * squares) & (lane[:1] < blocks)
+    count = jnp.sum(jnp.where(bad, 1.0, 0.0) + odd, axis=1, keepdims=True)
+    out_ref[...] = jnp.broadcast_to(jnp.where(lane[:1] == blocks, count, squares), out_ref.shape)
+
+
+def kernel(body, out_shape, in_specs, out_specs, flops=None):
+    cost = flops and pl.CostEstimate(flops=flops, bytes_accessed=2**19, transcendentals=0)
+    return pl.pallas_call(
+        body,
+        out_shape=out_shape,
+        in_specs=in_specs,
+        out_specs=out_specs,
+        compiler_params=PARAMS,
+        cost_estimate=cost,
+    )
+
+
+def to_groups(squares):
+    return lax.all_to_all(squares[:, None], GRP, split_axis=0, concat_axis=0, tiled=True)[:, 0]
+
+
+def exact_sums(own, blocks):
+    parts = lax.all_to_all(own, GRP, 0, 0, tiled=True)
+    summed = jnp.sum(parts.astype(jnp.float32), axis=0)
+    shape = jax.ShapeDtypeStruct((own.shape[0], HS), jnp.float32)
+    squares = kernel(functools.partial(squares_body, blocks), shape, [IN_VMEM], IN_VMEM)(summed)
+    return summed, squares
+
+
+def coded_sums(own):
+    groups, rows, width = own.shape
+    core = lax.axis_index("grp_1")
+    pairs = own.reshape(groups // 2, 2, rows, width)
+    give = lax.dynamic_index_in_dim(pairs, 1 - core, 1, keepdims=False)
+    keep = lax.dynamic_index_in_dim(pairs, core, 1, keepdims=False)
+    got = lax.ppermute(give, "grp_1", [(0, 1), (1, 0)])
+    sums = keep.astype(jnp.float32) + got.astype(jnp.float32)
+    shape = jax.ShapeDtypeStruct((groups // 2, rows, width // 2 + HS), jnp.int32)
+    words = kernel(pair_body, shape, [IN_VMEM], IN_VMEM)(sums)
+    words = lax.all_to_all(words, "grp_0", 0, 0, tiled=True)
+    shapes = (
+        jax.ShapeDtypeStruct((rows, width), jnp.float32),
+        jax.ShapeDtypeStruct((groups, HS), jnp.float32),
+    )
+    return kernel(gathered_body, shapes, [IN_VMEM], (IN_VMEM, IN_VMEM))(words)
+
+
+def shard_exchange(source, occupied, summed, squares):
+    rows = summed.shape[0]
+    peers = lax.axis_size(SHARD)
+    shape = jax.ShapeDtypeStruct((peers * (rows + 1), HS), jnp.int32)
+    specs = [IN_SMEM, IN_SMEM, IN_VMEM]
+    squares = to_groups(squares)
+    packed = kernel(functools.partial(packed_body, peers), shape, specs, IN_VMEM, 4 * 10**6)(source, occupied, summed)
+    body = functools.partial(outgoing_body, peers, rows)
+    outgoing = kernel(body, shape, [IN_VMEM, IN_VMEM], IN_VMEM)(packed, squares)
+    return lax.all_to_all(outgoing[:, None], SHARD, split_axis=0, concat_axis=0, tiled=True)[:, 0]
+
+
+def unpacked(arrived, wanted, *, blocks, rows, per_peer):
+    peers = arrived.shape[0] // (rows + 1)
+    shapes = (
+        jax.ShapeDtypeStruct((per_peer, peers, rows, HS), jnp.float32),
+        jax.ShapeDtypeStruct((per_peer,), jnp.float32),
+        jax.ShapeDtypeStruct((3,), jnp.float32),
+    )
+    body = functools.partial(arrived_body, peers, rows, blocks)
+    return kernel(body, shapes, [IN_VMEM, IN_VMEM], (IN_VMEM, IN_SMEM, IN_SMEM))(arrived, wanted)
+
+
 def per_device(partial_grads, joined_block, head_slot):
     own_rows = partial_grads[0]
     blocks = joined_block.shape[0]
@@ -145,45 +294,19 @@
     wanted = jnp.any(asked[:, :, None] & joined[None], axis=1).astype(jnp.float32)
     wanted = jnp.pad(wanted, ((0, 8 - wanted.shape[0]), (0, HS - blocks)))
 
-    parts = lax.all_to_all(own_rows.reshape(groups, rows, width), GRP, 0, 0, tiled=True)
-    summed = jnp.sum(parts.astype(jnp.float32), axis=0)
-
-    squares = pl.pallas_call(
-        functools.partial(squares_body, blocks),
-        out_shape=jax.ShapeDtypeStruct((groups, HS), jnp.float32),
-        in_specs=[IN_VMEM],
-        out_specs=IN_VMEM,
-        compiler_params=PARAMS,
-    )(summed)
-    squares = lax.all_to_all(squares[:, None], GRP, split_axis=0, concat_axis=0, tiled=True)[:, 0]
-    packed_shape = jax.ShapeDtypeStruct((peers * (rows + 1), HS), jnp.int32)
-    packed = pl.pallas_call(
-        functools.partial(packed_body, peers),
-        out_shape=packed_shape,
-        in_specs=[IN_SMEM, IN_SMEM, IN_VMEM],
-        out_specs=IN_VMEM,
-        compiler_params=PARAMS,
-        cost_estimate=pl.CostEstimate(flops=4 * 10**6, bytes_accessed=2**19, transcendentals=0),
-    )(source, occupied, summed)
-    outgoing = pl.pallas_call(
-        functools.partial(outgoing_body, peers, rows),
-        out_shape=packed_shape,
-        in_specs=[IN_VMEM, IN_VMEM],
-        out_specs=IN_VMEM,
-        compiler_params=PARAMS,
-    )(packed, squares)
-    arrived = lax.all_to_all(outgoing[:, None], SHARD, split_axis=0, concat_axis=0, tiled=True)
-    return pl.pallas_call(
-        functools.partial(arrived_body, peers, rows, blocks),
-        out_shape=(
-            jax.ShapeDtypeStruct((per_peer, peers, rows, HS), jnp.float32),
-            jax.ShapeDtypeStruct((per_peer,), jnp.float32),
-            jax.ShapeDtypeStruct((3,), jnp.float32),
-        ),
-        in_specs=[IN_VMEM, IN_VMEM],
-        out_specs=(IN_VMEM, IN_SMEM, IN_SMEM),
-        compiler_params=PARAMS,
-    )(arrived[:, 0], wanted)
+    finish = functools.partial(shard_exchange, source, occupied)
+    arrived = finish(*coded_sums(own_rows.reshape(groups, rows, width)))
+    body = functools.partial(count_body, peers, rows, blocks)
+    failed = kernel(body, jax.ShapeDtypeStruct((1,), jnp.float32), [IN_VMEM], IN_SMEM)(arrived)
+    unpack = functools.partial(unpacked, blocks=blocks, rows=rows, per_peer=per_peer)
+
+    def exactly(own, mine, weights):
+        return unpack(finish(*exact_sums(own, blocks)), weights)
+
+    def as_coded(own, mine, weights):
+        return unpack(mine, weights)
+
+    return lax.cond(failed[0] > 0.0, exactly, as_coded, own_rows.reshape(groups, rows, width), arrived, wanted)
 
 
 def solution(mesh):

time: 84.5 us -> 79.3 us (0.938)
  waiting for transfers between devices: 53.9 us -> 42.4 us
  Pallas kernels: 3.46 us -> 7.46 us
  local copies, waits for them, and re-layouts: 0.01 us -> 1.32 us
    all_to_all x3, waiting for transfers between devices: 53.9 us -> 40.1 us  [the longest x1 23.9 us: coded_sums(): words = lax.all_to_all(words, 'grp_0', 0, 0, tiled=True)]
    pallas_call x4 -> x6, Pallas kernels: 3.46 us -> 7.46 us  [the longest x1 2.99 us: coded_sums(): words = kernel(pair_body, shape, [IN_VMEM], IN_VMEM)(sums)]
    ppermute x0 -> x1, waiting for transfers between devices: none -> 2.25 us  [coded_sums(): got = lax.ppermute(give, 'grp_1', [(0, 1), (1, 0)])]
    ppermute x0 -> x1, starting transfers between devices: none -> 1.92 us  [coded_sums(): got = lax.ppermute(give, 'grp_1', [(0, 1), (1, 0)])]
    all_to_all x3, starting transfers between devices: 25.5 us -> 23.9 us  [the longest x1 10.3 us: coded_sums(): words = lax.all_to_all(words, 'grp_0', 0, 0, tiled=True)]
    squeeze x0 -> x1, local copies, waits for them, and re-layouts: none -> 1.3 us  [coded_sums(): give = lax.dynamic_index_in_dim(pairs, 1 - core, 1, keepdims=False)]
  transfers between devices with their start and end apart: 3 -> 4, of which waited for: 3 -> 4; matrix products, arithmetic and copies ran while one was open for 0% -> 0% of each run, Pallas kernels for 1% -> 1%
where the time goes in v5:
time: 79.3 us; the launch traced here: 79 us
  waiting for transfers between devices  42.4 us (53%)
  starting transfers between devices  25.9 us (33%)
  Pallas kernels  7.46 us (9%)
  between operations  1.4 us (2%)
  local copies, waits for them, and re-layouts  1.32 us (2%)
    all_to_all x1, waiting for transfers between devices, coded_sums(): words = lax.all_to_all(words, 'grp_0', 0, 0, tiled=True)  23.9 us
    all_to_all x1, starting transfers between devices, coded_sums(): words = lax.all_to_all(words, 'grp_0', 0, 0, tiled=True)  10.3 us
    all_to_all x1, starting transfers between devices, shard_exchange(): lax.all_to_all(outgoing[:, None], SHARD, split_axis=0, concat_axis=0, til...  10.2 us
    all_to_all x1, waiting for transfers between devices, shard_exchange(): lax.all_to_all(outgoing[:, None], SHARD, split_axis=0, concat_axis=0, til...  9.89 us
    all_to_all x1, waiting for transfers between devices, to_groups(): lax.all_to_all(squares[:, None], GRP, split_axis=0, concat_axis=0, tiled=...  6.3 us
    all_to_all x1, starting transfers between devices, to_groups(): lax.all_to_all(squares[:, None], GRP, split_axis=0, concat_axis=0, tiled=...  3.47 us
    pallas_call x1, Pallas kernels, coded_sums(): words = kernel(pair_body, shape, [IN_VMEM], IN_VMEM)(sums)  2.99 us
    ppermute x1, waiting for transfers between devices, coded_sums(): got = lax.ppermute(give, 'grp_1', [(0, 1), (1, 0)])  2.25 us
  transfers between devices with their start and end apart: 4, of which 4 were waited for; matrix products, arithmetic and copies ran while one was open for 0% of the time, Pallas kernels for 1%

profile of v5, /device:TPU:8, one launch (start us, length us, event | category | flops | bytes accessed | tf_op | source)
XLA Modules:
  0.0 79.0 jit_solution(3248962724510951947)
XLA Ops:
  0.6 0.0 copy-start
  0.6 1.3 %dynamic-slice_bitcast_fusion = bf16[8,8,6144]{2,1,0:T(8,128)(2,1)S(1)} fusion(bf16[8,2,8,6144]{3,2,1,0:T(8,128)(2,1)} %bitcast.30, s32[]{:T(128)S(6)} %select_n.8), kind=kLoop, calls=%fused_computation.2 | loop fusion | bytes 1572868 | tf_op jit(solution)/shard_map/jit(dynamic_index_in_dim)/squeeze | solution.py:236
  2.0 1.9 %collective-permute-start = (bf16[8,8,6144]{2,1,0:T(8,128)(2,1)S(1)}, bf16[8,8,6144]{2,1,0:T(8,128)(2,1)S(1)}, u32[]{:S(2)}, u32[]{:S(2)}) collective-permute-start(bf16[8,8,6144]{2,1,0:T(8,128)(2,1)S(1)} %dynamic-slice_bitcast_fusion), channel_id=1, source_target_pairs={{0,32},{32,0},{1,33},{33,1},{2,34},{34,2},{3,35},{35,3},{4,36},{36... | collective-permute-start | bytes 2359304 | tf_op jit(solution)/shard_map/ppermute | solution.py:238
  3.9 2.3 %collective-permute-done = bf16[8,8,6144]{2,1,0:T(8,128)(2,1)S(1)} collective-permute-done((bf16[8,8,6144]{2,1,0:T(8,128)(2,1)S(1)}, bf16[8,8,6144]{2,1,0:T(8,128)(2,1)S(1)}, u32[]{:S(2)}, u32[]{:S(2)}) %collective-permute-start) | collective-permute-done | bytes 786464 | tf_op jit(solution)/shard_map/ppermute | solution.py:238
  6.1 0.0 copy-done
  6.1 0.2 convert_add_fusion.sums_ref
  6.3 0.0 copy-start.2
  6.3 0.0 copy-start.1
  6.3 3.0 %shard_map.64 = s32[8,8,3200]{2,1,0:T(8,128)} custom-call(f32[8,8,6144]{2,1,0:T(8,128)S(1)} %convert_add_fusion.sums_ref), custom_call_target="tpu_custom_call" | custom-call | tf_op jit(solution)/shard_map/pallas_call | solution.py:241
  9.3 10.3 %all-to-all-start.3 = ((s32[8,8,3200]{2,1,0:T(8,128)}), s32[8,8,3200]{2,1,0:T(8,128)S(1)}, u32[]{:S(2)}, u32[]{:S(2)}) async-start(s32[8,8,3200]{2,1,0:T(8,128)} %shard_map.64), calls=%async_computation.3 | async-start | bytes 1638400 | tf_op jit(solution)/shard_map/all_to_all | solution.py:242
  19.7 0.0 copy-done.2
  19.7 0.1 broadcast_compare_fusion
  19.8 0.0 copy-done.1
  19.8 0.1 iota_compare_fusion
  19.8 23.9 %all-to-all-done.3.words_ref = s32[8,8,3200]{2,1,0:T(8,128)S(1)} async-done(((s32[8,8,3200]{2,1,0:T(8,128)}), s32[8,8,3200]{2,1,0:T(8,128)S(1)}, u32[]{:S(2)}, u32[]{:S(2)}) %all-to-all-start.3) | async-done | bytes 819232 | tf_op jit(solution)/shard_map/all_to_all | solution.py:242
  43.8 1.1 %shard_map.65 = (f32[8,6144]{1,0:T(8,128)S(1)}, f32[16,128]{1,0:T(8,128)}) custom-call(s32[8,8,3200]{2,1,0:T(8,128)S(1)} %all-to-all-done.3.words_ref), custom_call_target="tpu_custom_call" | custom-call | tf_op jit(solution)/shard_map/pallas_call | solution.py:247
  44.8 3.5 %all-to-all-start.4 = ((f32[16,1,128]{2,1,0:T(1,128)}), f32[16,1,128]{2,1,0:T(1,128)S(1)}, u32[]{:S(2)}, u32[]{:S(2)}) async-start(f32[16,1,128]{2,1,0:T(1,128)} %bitcast.13), calls=%async_computation.4 | async-start | bytes 16384 | tf_op jit(solution)/shard_map/all_to_all | solution.py:221
  48.3 0.1 convert_reduce_fusion.1
  48.4 1.1 %shard_map.66.packed_ref = s32[288,128]{1,0:T(8,128)S(1)} custom-call(s32[64]{0:T(128)S(1)} %get-tuple-element.36.source_ref, s32[64]{0:T(128)S(1)} %get-tuple-element.35.occupied_ref, f32[8,6144]{1,0:T(8,128)S(1)} %get-tuple-element.24.summed_ref), custom_call_target="tpu_custom_call" | custom-call | flops 4000000 | bytes 524288 | tf_op jit(solution)/shard_map/pallas_call | solution.py:256
  49.5 6.3 %all-to-all-done.4 = f32[16,1,128]{2,1,0:T(1,128)S(1)} async-done(((f32[16,1,128]{2,1,0:T(1,128)}), f32[16,1,128]{2,1,0:T(1,128)S(1)}, u32[]{:S(2)}, u32[]{:S(2)}) %all-to-all-start.4) | async-done | bytes 8224 | tf_op jit(solution)/shard_map/all_to_all | solution.py:221
  55.8 0.7 shard_map.67
  56.5 10.2 %all-to-all-start.5 = ((s32[288,1,128]{2,1,0:T(1,128)}), s32[288,1,128]{2,1,0:T(1,128)S(1)}, u32[]{:S(2)}, u32[]{:S(2)}) async-start(s32[288,1,128]{2,1,0:T(1,128)} %bitcast.16), calls=%async_computation.5 | async-start | bytes 294912 | tf_op jit(solution)/shard_map/all_to_all | solution.py:259
  66.7 0.1 and_reduce_fusion
  66.8 9.9 %all-to-all-done.5 = s32[288,1,128]{2,1,0:T(1,128)S(1)} async-done(((s32[288,1,128]{2,1,0:T(1,128)}), s32[288,1,128]{2,1,0:T(1,128)S(1)}, u32[]{:S(2)}, u32[]{:S(2)}) %all-to-all-start.5) | async-done | bytes 147488 | tf_op jit(solution)/shard_map/all_to_all | solution.py:259
  76.7 0.7 shard_map.68
  78.0 1.0 %conditional.1 = ((f32[2,32,8,128]{3,2,1,0:T(8,128)}, f32[2]{0:T(128)}, f32[3]{0:T(128)})) conditional(s32[]{:T(128)} %bitcast.18, (s32[288,128]{1,0:T(8,128)S(1)}, f32[8,128]{1,0:T(8,128)S(1)}) %tuple.27, (bf16[1,128,6144]{2,1,0:T(8,128)(2,1)S(1)}, s32[64]{0:T(128)S(1)}, s32[64]{0:T(128)S(1)}, f32[8,128]{1,0:T(8,128)S(1)}) %tuple.26), branch_computations={%region_3.4_spmd, %region_4.6_spmd} | conditional | flops 5523712 | bytes 5759016 | solution.py:309
  78.0 1.0 %branch_0_fun.1 = (f32[2,32,8,128]{3,2,1,0:T(8,128)}, f32[2]{0:T(128)}, f32[3]{0:T(128)}) custom-call(s32[288,128]{1,0:T(8,128)S(1)} %get-tuple-element.13.arrived_ref, f32[8,128]{1,0:T(8,128)S(1)} %get-tuple-element.14.wanted_ref), custom_call_target="tpu_custom_call" | custom-call | tf_op jit(solution)/shard_map/cond/branch_0_fun/pallas_call | solution.py:270
  (5 shorter events, 0.0 us)
Async XLA Ops:
  0.6 5.5 %copy-start = (bf16[1,128,6144]{2,1,0:T(8,128)(2,1)S(1)}, bf16[1,128,6144]{2,1,0:T(8,128)(2,1)}, u32[]{:S(2)}) copy-start(bf16[1,128,6144]{2,1,0:T(8,128)(2,1)} %param.5) | copy-start | bytes 4718596
  2.0 4.2 %collective-permute-start = (bf16[8,8,6144]{2,1,0:T(8,128)(2,1)S(1)}, bf16[8,8,6144]{2,1,0:T(8,128)(2,1)S(1)}, u32[]{:S(2)}, u32[]{:S(2)}) collective-permute-start(bf16[8,8,6144]{2,1,0:T(8,128)(2,1)S(1)} %dynamic-slice_bitcast_fusion), channel_id=1, source_target_pairs={{0,32},{32,0},{1,33},{33,1},{2,34},{34,2},{3,35},{35,3},{4,36},{36... | collective-permute-start | bytes 2359304 | tf_op jit(solution)/shard_map/ppermute | solution.py:238
  6.3 13.4 %copy-start.2 = (s32[48]{0:T(128)S(1)}, s32[48]{0:T(128)}, u32[]{:S(2)}) copy-start(s32[48]{0:T(128)} %param.7) | copy-start | bytes 580
  6.3 13.4 %copy-start.1 = (s32[48]{0:T(128)S(1)}, s32[48]{0:T(128)}, u32[]{:S(2)}) copy-start(s32[48]{0:T(128)} %param.6) | copy-start | bytes 580
  9.3 34.4 %all-to-all-start.3 = ((s32[8,8,3200]{2,1,0:T(8,128)}), s32[8,8,3200]{2,1,0:T(8,128)S(1)}, u32[]{:S(2)}, u32[]{:S(2)}) async-start(s32[8,8,3200]{2,1,0:T(8,128)} %shard_map.64), calls=%async_computation.3 | async-start | bytes 1638400 | tf_op jit(solution)/shard_map/all_to_all | solution.py:242
  44.8 10.9 %all-to-all-start.4 = ((f32[16,1,128]{2,1,0:T(1,128)}), f32[16,1,128]{2,1,0:T(1,128)S(1)}, u32[]{:S(2)}, u32[]{:S(2)}) async-start(f32[16,1,128]{2,1,0:T(1,128)} %bitcast.13), calls=%async_computation.4 | async-start | bytes 16384 | tf_op jit(solution)/shard_map/all_to_all | solution.py:221
  56.5 20.2 %all-to-all-start.5 = ((s32[288,1,128]{2,1,0:T(1,128)}), s32[288,1,128]{2,1,0:T(1,128)S(1)}, u32[]{:S(2)}, u32[]{:S(2)}) async-start(s32[288,1,128]{2,1,0:T(1,128)} %bitcast.16), calls=%async_computation.5 | async-start | bytes 294912 | tf_op jit(solution)/shard_map/all_to_all | solution.py:259

commit v6 on v5

--- a/solution.py
+++ b/solution.py
@@ -59,13 +59,6 @@
     return ((words & 1023) - 512).astype(jnp.float32)
 
 
-def count_body(peers, rows, blocks, arrived_ref, out_ref):
-    riders = [arrived_ref[pl.ds(peer * (rows + 1) + rows, 1), :] for peer in range(peers)]
-    riders = jnp.concatenate(riders, axis=0)
-    lane = lax.broadcasted_iota(jnp.int32, riders.shape, 1)
-    out_ref[0] = jnp.sum(jnp.where((lane == blocks) & (riders != 0), 1.0, 0.0))
-
-
 def value_of(words):
     up = halves(exponent_of(words))
     return mantissa_of(words) * up * up
@@ -106,12 +99,13 @@
         out_ref[pl.ds(start + rows, 1), :] = packed_ref[pl.ds(start + rows, 1), :] + words
 
 
-def arrived_body(peers, rows, blocks, arrived_ref, wanted_ref, owned_ref, head_ref, type_ref):
+def arrived_body(peers, rows, blocks, arrived_ref, wanted_ref, owned_ref, head_ref, type_ref, failed_ref):
     riders = [arrived_ref[pl.ds(peer * (rows + 1) + rows, 1), :] for peer in range(peers)]
     riders = jnp.concatenate(riders, axis=0)
     mantissa = mantissa_of(riders)
     up = halves(exponent_of(riders))
     lanes = lax.broadcasted_iota(jnp.int32, riders.shape, 1)
+    failed_ref[0] = jnp.sum(jnp.where((lanes == blocks) & (riders != 0), 1.0, 0.0))
     total = jnp.sum(jnp.where(lanes < blocks, mantissa * up * up, 0.0), axis=0, keepdims=True)
     sums = jnp.sum(wanted_ref[...] * total, axis=1, keepdims=True)
     at = lax.broadcasted_iota(jnp.int32, sums.shape, 0)
@@ -143,26 +137,27 @@
     half = width // 2
     lane = lax.broadcasted_iota(jnp.int32, (rows, HS), 1)
 
-    def chunk_step(chunk, _):
+    def tile(chunk, place):
+        return sums_ref[chunk, :, pl.ds(place * HS, HS)]
+
+    gains = []
+    for chunk in range(chunks):
         most = jnp.zeros((rows, HS), jnp.float32)
         for span in range(width // (SPAN * HS)):
-            tiles = [sums_ref[chunk, :, pl.ds((SPAN * span + nth) * HS, HS)] for nth in range(SPAN)]
-            peak = functools.reduce(jnp.maximum, [jnp.abs(tile) for tile in tiles])
-            most = jnp.where(lane == span, jnp.max(peak, axis=1, keepdims=True), most)
+            peaks = [jnp.abs(tile(chunk, SPAN * span + nth)) for nth in range(SPAN)]
+            peak = jnp.max(functools.reduce(jnp.maximum, peaks), axis=1, keepdims=True)
+            most = jnp.where(lane == span, peak, most)
         words, _ = words_of(jnp.minimum(most, 2.0 * HIGHEST))
         out_ref[chunk, :, pl.ds(half, HS)] = words
-        gain = jnp.where(words > 0, 32767.0 / jnp.maximum(value_of(words), LOWEST * 0.5), 0.0)
-        spans = width // (SPAN * HS)
-        gains = [jnp.broadcast_to(gain[:, span : span + 1], (rows, HS)) for span in range(spans)]
+        gains.append(jnp.where(words > 0, 32767.0 / jnp.maximum(value_of(words), LOWEST * 0.5), 0.0))
+    for chunk in range(chunks):
         for block in range(half // HS):
             codes = []
             for place in (block, block + half // HS):
-                tile = sums_ref[chunk, :, pl.ds(place * HS, HS)]
-                codes.append(jnp.floor(tile * gains[place // SPAN] + 0.5).astype(jnp.int32))
+                span = place // SPAN
+                value = tile(chunk, place) * gains[chunk][:, span : span + 1]
+                codes.append(jnp.floor(value + 0.5).astype(jnp.int32))
             out_ref[chunk, :, pl.ds(block * HS, HS)] = (codes[0] << 16) | (codes[1] & 65535)
-        return 0
-
-    lax.fori_loop(0, chunks, chunk_step, 0)
 
 
 def gathered_body(words_ref, summed_ref, out_ref):
@@ -265,9 +260,11 @@
         jax.ShapeDtypeStruct((per_peer, peers, rows, HS), jnp.float32),
         jax.ShapeDtypeStruct((per_peer,), jnp.float32),
         jax.ShapeDtypeStruct((3,), jnp.float32),
+        jax.ShapeDtypeStruct((1,), jnp.float32),
     )
     body = functools.partial(arrived_body, peers, rows, blocks)
-    return kernel(body, shapes, [IN_VMEM, IN_VMEM], (IN_VMEM, IN_SMEM, IN_SMEM))(arrived, wanted)
+    specs = (IN_VMEM, IN_SMEM, IN_SMEM, IN_SMEM)
+    return kernel(body, shapes, [IN_VMEM, IN_VMEM], specs)(arrived, wanted)
 
 
 def per_device(partial_grads, joined_block, head_slot):
@@ -296,17 +293,14 @@
 
     finish = functools.partial(shard_exchange, source, occupied)
     arrived = finish(*coded_sums(own_rows.reshape(groups, rows, width)))
-    body = functools.partial(count_body, peers, rows, blocks)
-    failed = kernel(body, jax.ShapeDtypeStruct((1,), jnp.float32), [IN_VMEM], IN_SMEM)(arrived)
-    unpack = functools.partial(unpacked, blocks=blocks, rows=rows, per_peer=per_peer)
-
-    def exactly(own, mine, weights):
-        return unpack(finish(*exact_sums(own, blocks)), weights)
-
-    def as_coded(own, mine, weights):
-        return unpack(mine, weights)
-
-    return lax.cond(failed[0] > 0.0, exactly, as_coded, own_rows.reshape(groups, rows, width), arrived, wanted)
+    unpack = functools.partial(unpacked, wanted=wanted, blocks=blocks, rows=rows, per_peer=per_peer)
+
+    def exactly(state):
+        own = jnp.where(state[3][0] > 0.0, own_rows, jnp.zeros_like(own_rows))
+        return unpack(finish(*exact_sums(own.reshape(groups, rows, width), blocks)))
+
+    results = lax.while_loop(lambda state: state[3][0] > 0.0, exactly, unpack(arrived))
+    return results[:3]
 
 
 def solution(mesh):

time: 79.3 us -> 77.2 us (0.974)
  Pallas kernels: 7.46 us -> 5.28 us
    pallas_call x1, Pallas kernels: 2.99 us -> 1.45 us  [coded_sums(): words = kernel(pair_body, shape, [IN_VMEM], IN_VMEM)(sums)]
    pallas_call x2 -> x1, Pallas kernels: 1.62 us -> 0.98 us  [unpacked(): return kernel(body, shapes, [IN_VMEM, IN_VMEM], specs)(arrived, wanted)]
  transfers between devices with their start and end apart: 4 -> 4, of which waited for: 4 -> 4; matrix products, arithmetic and copies ran while one was open for 0% -> 1% of each run, Pallas kernels for 1% -> 1%
where the time goes in v6:
time: 77.2 us; the launch traced here: 76.8 us
  waiting for transfers between devices  42.4 us (55%)
  starting transfers between devices  25.9 us (34%)
  Pallas kernels  5.28 us (7%)
  local copies, waits for them, and re-layouts  1.32 us (2%)
    all_to_all x1, waiting for transfers between devices, coded_sums(): words = lax.all_to_all(words, 'grp_0', 0, 0, tiled=True)  23.9 us
    all_to_all x1, starting transfers between devices, coded_sums(): words = lax.all_to_all(words, 'grp_0', 0, 0, tiled=True)  10.3 us
    all_to_all x1, starting transfers between devices, shard_exchange(): lax.all_to_all(outgoing[:, None], SHARD, split_axis=0, concat_axis=0, til...  10.2 us
    all_to_all x1, waiting for transfers between devices, shard_exchange(): lax.all_to_all(outgoing[:, None], SHARD, split_axis=0, concat_axis=0, til...  9.89 us
    all_to_all x1, waiting for transfers between devices, to_groups(): lax.all_to_all(squares[:, None], GRP, split_axis=0, concat_axis=0, tiled=...  6.3 us
    all_to_all x1, starting transfers between devices, to_groups(): lax.all_to_all(squares[:, None], GRP, split_axis=0, concat_axis=0, tiled=...  3.47 us
    ppermute x1, waiting for transfers between devices, coded_sums(): got = lax.ppermute(give, 'grp_1', [(0, 1), (1, 0)])  2.25 us
    ppermute x1, starting transfers between devices, coded_sums(): got = lax.ppermute(give, 'grp_1', [(0, 1), (1, 0)])  1.92 us
  transfers between devices with their start and end apart: 4, of which 4 were waited for; matrix products, arithmetic and copies ran while one was open for 1% of the time, Pallas kernels for 1%

profile of v6, /device:TPU:8, one launch (start us, length us, event | category | flops | bytes accessed | tf_op | source)
XLA Modules:
  0.0 76.8 jit_solution(1017561472593614380)
XLA Ops:
  0.6 0.0 copy-start
  0.6 1.3 %dynamic-slice_bitcast_fusion = bf16[8,8,6144]{2,1,0:T(8,128)(2,1)S(1)} fusion(bf16[8,2,8,6144]{3,2,1,0:T(8,128)(2,1)} %bitcast.41, s32[]{:T(128)S(6)} %select_n.20), kind=kLoop, calls=%fused_computation.3 | loop fusion | bytes 1572868 | tf_op jit(solution)/shard_map/jit(dynamic_index_in_dim)/squeeze | solution.py:231
  2.0 1.9 %collective-permute-start = (bf16[8,8,6144]{2,1,0:T(8,128)(2,1)S(1)}, bf16[8,8,6144]{2,1,0:T(8,128)(2,1)S(1)}, u32[]{:S(2)}, u32[]{:S(2)}) collective-permute-start(bf16[8,8,6144]{2,1,0:T(8,128)(2,1)S(1)} %dynamic-slice_bitcast_fusion), channel_id=1, source_target_pairs={{0,32},{32,0},{1,33},{33,1},{2,34},{34,2},{3,35},{35,3},{4,36},{36... | collective-permute-start | bytes 2359304 | tf_op jit(solution)/shard_map/ppermute | solution.py:233
  3.9 2.3 %collective-permute-done = bf16[8,8,6144]{2,1,0:T(8,128)(2,1)S(1)} collective-permute-done((bf16[8,8,6144]{2,1,0:T(8,128)(2,1)S(1)}, bf16[8,8,6144]{2,1,0:T(8,128)(2,1)S(1)}, u32[]{:S(2)}, u32[]{:S(2)}) %collective-permute-start) | collective-permute-done | bytes 786464 | tf_op jit(solution)/shard_map/ppermute | solution.py:233
  6.1 0.0 copy-done
  6.1 0.2 convert_add_fusion.sums_ref
  6.3 0.0 copy-start.2
  6.3 0.0 copy-start.1
  6.3 1.4 %shard_map.58 = s32[8,8,3200]{2,1,0:T(8,128)} custom-call(f32[8,8,6144]{2,1,0:T(8,128)S(1)} %convert_add_fusion.sums_ref), custom_call_target="tpu_custom_call" | custom-call | tf_op jit(solution)/shard_map/pallas_call | solution.py:236
  7.8 10.3 %all-to-all-start.3 = ((s32[8,8,3200]{2,1,0:T(8,128)}), s32[8,8,3200]{2,1,0:T(8,128)S(1)}, u32[]{:S(2)}, u32[]{:S(2)}) async-start(s32[8,8,3200]{2,1,0:T(8,128)} %shard_map.58), calls=%async_computation.3 | async-start | bytes 1638400 | tf_op jit(solution)/shard_map/all_to_all | solution.py:237
  18.1 0.0 copy-done.2
  18.1 0.1 broadcast_compare_fusion
  18.2 0.0 copy-done.1
  18.2 0.1 iota_compare_fusion
  18.3 23.9 %all-to-all-done.3.words_ref = s32[8,8,3200]{2,1,0:T(8,128)S(1)} async-done(((s32[8,8,3200]{2,1,0:T(8,128)}), s32[8,8,3200]{2,1,0:T(8,128)S(1)}, u32[]{:S(2)}, u32[]{:S(2)}) %all-to-all-start.3) | async-done | bytes 819232 | tf_op jit(solution)/shard_map/all_to_all | solution.py:237
  42.2 1.1 %shard_map.59 = (f32[8,6144]{1,0:T(8,128)S(1)}, f32[16,128]{1,0:T(8,128)}) custom-call(s32[8,8,3200]{2,1,0:T(8,128)S(1)} %all-to-all-done.3.words_ref), custom_call_target="tpu_custom_call" | custom-call | tf_op jit(solution)/shard_map/pallas_call | solution.py:242
  43.3 3.5 %all-to-all-start.4 = ((f32[16,1,128]{2,1,0:T(1,128)}), f32[16,1,128]{2,1,0:T(1,128)S(1)}, u32[]{:S(2)}, u32[]{:S(2)}) async-start(f32[16,1,128]{2,1,0:T(1,128)} %bitcast.15), calls=%async_computation.4 | async-start | bytes 16384 | tf_op jit(solution)/shard_map/all_to_all | solution.py:216
  46.8 0.1 convert_reduce_fusion.1
  46.9 1.1 %shard_map.60.packed_ref = s32[288,128]{1,0:T(8,128)S(1)} custom-call(s32[64]{0:T(128)S(1)} %get-tuple-element.128.source_ref, s32[64]{0:T(128)S(1)} %get-tuple-element.129.occupied_ref, f32[8,6144]{1,0:T(8,128)S(1)} %get-tuple-element.54.summed_ref), custom_call_target="tpu_custom_call" | custom-call | flops 4000000 | bytes 524288 | tf_op jit(solution)/shard_map/pallas_call | solution.py:251
  47.9 6.3 %all-to-all-done.4 = f32[16,1,128]{2,1,0:T(1,128)S(1)} async-done(((f32[16,1,128]{2,1,0:T(1,128)}), f32[16,1,128]{2,1,0:T(1,128)S(1)}, u32[]{:S(2)}, u32[]{:S(2)}) %all-to-all-start.4) | async-done | bytes 8224 | tf_op jit(solution)/shard_map/all_to_all | solution.py:216
  54.2 0.7 shard_map.61
  54.9 10.2 %all-to-all-start.5 = ((s32[288,1,128]{2,1,0:T(1,128)}), s32[288,1,128]{2,1,0:T(1,128)S(1)}, u32[]{:S(2)}, u32[]{:S(2)}) async-start(s32[288,1,128]{2,1,0:T(1,128)} %bitcast.18), calls=%async_computation.5 | async-start | bytes 294912 | tf_op jit(solution)/shard_map/all_to_all | solution.py:254
  65.1 0.1 and_reduce_fusion
  65.3 9.9 %all-to-all-done.5 = s32[288,1,128]{2,1,0:T(1,128)S(1)} async-done(((s32[288,1,128]{2,1,0:T(1,128)}), s32[288,1,128]{2,1,0:T(1,128)S(1)}, u32[]{:S(2)}, u32[]{:S(2)}) %all-to-all-start.5) | async-done | bytes 147488 | tf_op jit(solution)/shard_map/all_to_all | solution.py:254
  75.2 1.0 %shard_map.62 = (f32[2,32,8,128]{3,2,1,0:T(8,128)}, f32[2]{0:T(128)}, f32[3]{0:T(128)}, f32[1]{0:T(128)}) custom-call(s32[288,128]{1,0:T(8,128)S(1)} %bitcast.39, f32[8,128]{1,0:T(8,128)S(1)} %pad_convert_fusion.wanted_ref), custom_call_target="tpu_custom_call" | custom-call | tf_op jit(solution)/shard_map/pallas_call | solution.py:267
  76.1 0.7 while.14
  (5 shorter events, 0.0 us)
Async XLA Ops:
  0.6 5.5 %copy-start = (bf16[1,128,6144]{2,1,0:T(8,128)(2,1)S(1)}, bf16[1,128,6144]{2,1,0:T(8,128)(2,1)}, u32[]{:S(2)}) copy-start(bf16[1,128,6144]{2,1,0:T(8,128)(2,1)} %param.5) | copy-start | bytes 4718596
  2.0 4.2 %collective-permute-start = (bf16[8,8,6144]{2,1,0:T(8,128)(2,1)S(1)}, bf16[8,8,6144]{2,1,0:T(8,128)(2,1)S(1)}, u32[]{:S(2)}, u32[]{:S(2)}) collective-permute-start(bf16[8,8,6144]{2,1,0:T(8,128)(2,1)S(1)} %dynamic-slice_bitcast_fusion), channel_id=1, source_target_pairs={{0,32},{32,0},{1,33},{33,1},{2,34},{34,2},{3,35},{35,3},{4,36},{36... | collective-permute-start | bytes 2359304 | tf_op jit(solution)/shard_map/ppermute | solution.py:233
  6.3 11.8 %copy-start.2 = (s32[48]{0:T(128)S(1)}, s32[48]{0:T(128)}, u32[]{:S(2)}) copy-start(s32[48]{0:T(128)} %param.7) | copy-start | bytes 580
  6.3 11.9 %copy-start.1 = (s32[48]{0:T(128)S(1)}, s32[48]{0:T(128)}, u32[]{:S(2)}) copy-start(s32[48]{0:T(128)} %param.6) | copy-start | bytes 580
  7.8 34.4 %all-to-all-start.3 = ((s32[8,8,3200]{2,1,0:T(8,128)}), s32[8,8,3200]{2,1,0:T(8,128)S(1)}, u32[]{:S(2)}, u32[]{:S(2)}) async-start(s32[8,8,3200]{2,1,0:T(8,128)} %shard_map.58), calls=%async_computation.3 | async-start | bytes 1638400 | tf_op jit(solution)/shard_map/all_to_all | solution.py:237
  43.3 10.9 %all-to-all-start.4 = ((f32[16,1,128]{2,1,0:T(1,128)}), f32[16,1,128]{2,1,0:T(1,128)S(1)}, u32[]{:S(2)}, u32[]{:S(2)}) async-start(f32[16,1,128]{2,1,0:T(1,128)} %bitcast.15), calls=%async_computation.4 | async-start | bytes 16384 | tf_op jit(solution)/shard_map/all_to_all | solution.py:216
  54.9 20.2 %all-to-all-start.5 = ((s32[288,1,128]{2,1,0:T(1,128)}), s32[288,1,128]{2,1,0:T(1,128)S(1)}, u32[]{:S(2)}, u32[]{:S(2)}) async-start(s32[288,1,128]{2,1,0:T(1,128)} %bitcast.18), calls=%async_computation.5 | async-start | bytes 294912 | tf_op jit(solution)/shard_map/all_to_all | solution.py:254

commit v7 on v6

--- a/solution.py
+++ b/solution.py
@@ -15,8 +15,8 @@
 SHARD = ("shard_0", "shard_1")
 GRP = ("grp_0", "grp_1")
 SCALES = 64
-NOISE = 1.5e-4
-SPAN = 4
+NOISE = 1e-4
+SPAN = 2
 LOWEST = 1e-18
 HIGHEST = 1e8
 LIFT = 2.0**30

time: 77.2 us -> 77.4 us (level)
  no operation moved by 1% of the time
where the time goes in v7:
time: 77.4 us; the launch traced here: 77.1 us
  waiting for transfers between devices  42.4 us (55%)
  starting transfers between devices  25.9 us (33%)
  Pallas kernels  5.54 us (7%)
  local copies, waits for them, and re-layouts  1.32 us (2%)
    all_to_all x1, waiting for transfers between devices, coded_sums(): words = lax.all_to_all(words, 'grp_0', 0, 0, tiled=True)  23.9 us
    all_to_all x1, starting transfers between devices, coded_sums(): words = lax.all_to_all(words, 'grp_0', 0, 0, tiled=True)  10.3 us
    all_to_all x1, starting transfers between devices, shard_exchange(): lax.all_to_all(outgoing[:, None], SHARD, split_axis=0, concat_axis=0, til...  10.2 us
    all_to_all x1, waiting for transfers between devices, shard_exchange(): lax.all_to_all(outgoing[:, None], SHARD, split_axis=0, concat_axis=0, til...  9.89 us
    all_to_all x1, waiting for transfers between devices, to_groups(): lax.all_to_all(squares[:, None], GRP, split_axis=0, concat_axis=0, tiled=...  6.3 us
    all_to_all x1, starting transfers between devices, to_groups(): lax.all_to_all(squares[:, None], GRP, split_axis=0, concat_axis=0, tiled=...  3.47 us
    ppermute x1, waiting for transfers between devices, coded_sums(): got = lax.ppermute(give, 'grp_1', [(0, 1), (1, 0)])  2.25 us
    ppermute x1, starting transfers between devices, coded_sums(): got = lax.ppermute(give, 'grp_1', [(0, 1), (1, 0)])  1.92 us
  transfers between devices with their start and end apart: 4, of which 4 were waited for; matrix products, arithmetic and copies ran while one was open for 1% of the time, Pallas kernels for 1%

profile of v7, /device:TPU:8, one launch (start us, length us, event | category | flops | bytes accessed | tf_op | source)
XLA Modules:
  0.0 77.1 jit_solution(12859592022449164363)
XLA Ops:
  0.6 0.0 copy-start
  0.6 1.3 %dynamic-slice_bitcast_fusion = bf16[8,8,6144]{2,1,0:T(8,128)(2,1)S(1)} fusion(bf16[8,2,8,6144]{3,2,1,0:T(8,128)(2,1)} %bitcast.41, s32[]{:T(128)S(6)} %select_n.20), kind=kLoop, calls=%fused_computation.3 | loop fusion | bytes 1572868 | tf_op jit(solution)/shard_map/jit(dynamic_index_in_dim)/squeeze | solution.py:231
  2.0 1.9 %collective-permute-start = (bf16[8,8,6144]{2,1,0:T(8,128)(2,1)S(1)}, bf16[8,8,6144]{2,1,0:T(8,128)(2,1)S(1)}, u32[]{:S(2)}, u32[]{:S(2)}) collective-permute-start(bf16[8,8,6144]{2,1,0:T(8,128)(2,1)S(1)} %dynamic-slice_bitcast_fusion), channel_id=1, source_target_pairs={{0,32},{32,0},{1,33},{33,1},{2,34},{34,2},{3,35},{35,3},{4,36},{36... | collective-permute-start | bytes 2359304 | tf_op jit(solution)/shard_map/ppermute | solution.py:233
  3.9 2.3 %collective-permute-done = bf16[8,8,6144]{2,1,0:T(8,128)(2,1)S(1)} collective-permute-done((bf16[8,8,6144]{2,1,0:T(8,128)(2,1)S(1)}, bf16[8,8,6144]{2,1,0:T(8,128)(2,1)S(1)}, u32[]{:S(2)}, u32[]{:S(2)}) %collective-permute-start) | collective-permute-done | bytes 786464 | tf_op jit(solution)/shard_map/ppermute | solution.py:233
  6.1 0.0 copy-done
  6.1 0.2 convert_add_fusion.sums_ref
  6.3 0.0 copy-start.2
  6.3 0.0 copy-start.1
  6.3 1.6 %shard_map.58 = s32[8,8,3200]{2,1,0:T(8,128)} custom-call(f32[8,8,6144]{2,1,0:T(8,128)S(1)} %convert_add_fusion.sums_ref), custom_call_target="tpu_custom_call" | custom-call | tf_op jit(solution)/shard_map/pallas_call | solution.py:236
  7.9 10.3 %all-to-all-start.3 = ((s32[8,8,3200]{2,1,0:T(8,128)}), s32[8,8,3200]{2,1,0:T(8,128)S(1)}, u32[]{:S(2)}, u32[]{:S(2)}) async-start(s32[8,8,3200]{2,1,0:T(8,128)} %shard_map.58), calls=%async_computation.3 | async-start | bytes 1638400 | tf_op jit(solution)/shard_map/all_to_all | solution.py:237
  18.2 0.0 copy-done.2
  18.3 0.1 broadcast_compare_fusion
  18.3 0.0 copy-done.1
  18.3 0.1 iota_compare_fusion
  18.4 23.9 %all-to-all-done.3.words_ref = s32[8,8,3200]{2,1,0:T(8,128)S(1)} async-done(((s32[8,8,3200]{2,1,0:T(8,128)}), s32[8,8,3200]{2,1,0:T(8,128)S(1)}, u32[]{:S(2)}, u32[]{:S(2)}) %all-to-all-start.3) | async-done | bytes 819232 | tf_op jit(solution)/shard_map/all_to_all | solution.py:237
  42.3 1.2 %shard_map.59 = (f32[8,6144]{1,0:T(8,128)S(1)}, f32[16,128]{1,0:T(8,128)}) custom-call(s32[8,8,3200]{2,1,0:T(8,128)S(1)} %all-to-all-done.3.words_ref), custom_call_target="tpu_custom_call" | custom-call | tf_op jit(solution)/shard_map/pallas_call | solution.py:242
  43.6 3.5 %all-to-all-start.4 = ((f32[16,1,128]{2,1,0:T(1,128)}), f32[16,1,128]{2,1,0:T(1,128)S(1)}, u32[]{:S(2)}, u32[]{:S(2)}) async-start(f32[16,1,128]{2,1,0:T(1,128)} %bitcast.15), calls=%async_computation.4 | async-start | bytes 16384 | tf_op jit(solution)/shard_map/all_to_all | solution.py:216
  47.0 0.1 convert_reduce_fusion.1
  47.1 1.1 %shard_map.60.packed_ref = s32[288,128]{1,0:T(8,128)S(1)} custom-call(s32[64]{0:T(128)S(1)} %get-tuple-element.128.source_ref, s32[64]{0:T(128)S(1)} %get-tuple-element.129.occupied_ref, f32[8,6144]{1,0:T(8,128)S(1)} %get-tuple-element.54.summed_ref), custom_call_target="tpu_custom_call" | custom-call | flops 4000000 | bytes 524288 | tf_op jit(solution)/shard_map/pallas_call | solution.py:251
  48.2 6.3 %all-to-all-done.4 = f32[16,1,128]{2,1,0:T(1,128)S(1)} async-done(((f32[16,1,128]{2,1,0:T(1,128)}), f32[16,1,128]{2,1,0:T(1,128)S(1)}, u32[]{:S(2)}, u32[]{:S(2)}) %all-to-all-start.4) | async-done | bytes 8224 | tf_op jit(solution)/shard_map/all_to_all | solution.py:216
  54.5 0.7 shard_map.61
  55.2 10.2 %all-to-all-start.5 = ((s32[288,1,128]{2,1,0:T(1,128)}), s32[288,1,128]{2,1,0:T(1,128)S(1)}, u32[]{:S(2)}, u32[]{:S(2)}) async-start(s32[288,1,128]{2,1,0:T(1,128)} %bitcast.18), calls=%async_computation.5 | async-start | bytes 294912 | tf_op jit(solution)/shard_map/all_to_all | solution.py:254
  65.4 0.1 and_reduce_fusion
  65.5 9.9 %all-to-all-done.5 = s32[288,1,128]{2,1,0:T(1,128)S(1)} async-done(((s32[288,1,128]{2,1,0:T(1,128)}), s32[288,1,128]{2,1,0:T(1,128)S(1)}, u32[]{:S(2)}, u32[]{:S(2)}) %all-to-all-start.5) | async-done | bytes 147488 | tf_op jit(solution)/shard_map/all_to_all | solution.py:254
  75.4 1.0 %shard_map.62 = (f32[2,32,8,128]{3,2,1,0:T(8,128)}, f32[2]{0:T(128)}, f32[3]{0:T(128)}, f32[1]{0:T(128)}) custom-call(s32[288,128]{1,0:T(8,128)S(1)} %bitcast.39, f32[8,128]{1,0:T(8,128)S(1)} %pad_convert_fusion.wanted_ref), custom_call_target="tpu_custom_call" | custom-call | tf_op jit(solution)/shard_map/pallas_call | solution.py:267
  76.4 0.7 while.14
  (5 shorter events, 0.0 us)
Async XLA Ops:
  0.6 5.5 %copy-start = (bf16[1,128,6144]{2,1,0:T(8,128)(2,1)S(1)}, bf16[1,128,6144]{2,1,0:T(8,128)(2,1)}, u32[]{:S(2)}) copy-start(bf16[1,128,6144]{2,1,0:T(8,128)(2,1)} %param.5) | copy-start | bytes 4718596
  2.0 4.2 %collective-permute-start = (bf16[8,8,6144]{2,1,0:T(8,128)(2,1)S(1)}, bf16[8,8,6144]{2,1,0:T(8,128)(2,1)S(1)}, u32[]{:S(2)}, u32[]{:S(2)}) collective-permute-start(bf16[8,8,6144]{2,1,0:T(8,128)(2,1)S(1)} %dynamic-slice_bitcast_fusion), channel_id=1, source_target_pairs={{0,32},{32,0},{1,33},{33,1},{2,34},{34,2},{3,35},{35,3},{4,36},{36... | collective-permute-start | bytes 2359304 | tf_op jit(solution)/shard_map/ppermute | solution.py:233
  6.3 11.9 %copy-start.2 = (s32[48]{0:T(128)S(1)}, s32[48]{0:T(128)}, u32[]{:S(2)}) copy-start(s32[48]{0:T(128)} %param.7) | copy-start | bytes 580
  6.3 12.0 %copy-start.1 = (s32[48]{0:T(128)S(1)}, s32[48]{0:T(128)}, u32[]{:S(2)}) copy-start(s32[48]{0:T(128)} %param.6) | copy-start | bytes 580
  7.9 34.4 %all-to-all-start.3 = ((s32[8,8,3200]{2,1,0:T(8,128)}), s32[8,8,3200]{2,1,0:T(8,128)S(1)}, u32[]{:S(2)}, u32[]{:S(2)}) async-start(s32[8,8,3200]{2,1,0:T(8,128)} %shard_map.58), calls=%async_computation.3 | async-start | bytes 1638400 | tf_op jit(solution)/shard_map/all_to_all | solution.py:237
  43.6 10.9 %all-to-all-start.4 = ((f32[16,1,128]{2,1,0:T(1,128)}), f32[16,1,128]{2,1,0:T(1,128)S(1)}, u32[]{:S(2)}, u32[]{:S(2)}) async-start(f32[16,1,128]{2,1,0:T(1,128)} %bitcast.15), calls=%async_computation.4 | async-start | bytes 16384 | tf_op jit(solution)/shard_map/all_to_all | solution.py:216
  55.2 20.2 %all-to-all-start.5 = ((s32[288,1,128]{2,1,0:T(1,128)}), s32[288,1,128]{2,1,0:T(1,128)S(1)}, u32[]{:S(2)}, u32[]{:S(2)}) async-start(s32[288,1,128]{2,1,0:T(1,128)} %bitcast.18), calls=%async_computation.5 | async-start | bytes 294912 | tf_op jit(solution)/shard_map/all_to_all | solution.py:254
